TPU v7x, 32 devices: a whole 2x2x4 slice. The times are simulated.
32 devices in a mesh: group: 4 (over z), batch: 8 (over y, x, core).
Axes of the slice: x: 2, y: 2, z: 4, core: 2. Of those that a mesh axis runs over, the one named last changes fastest.
Arguments:
- embeds: bfloat16 [65536, 256], P(('group', 'batch')), may hold values from -6 to 6
- out_grad: bfloat16 [65536, 256], P(('group', 'batch')), may hold values from -48 to 48
- w_query: bfloat16 [256, 256], replicated, may hold values from -0.375 to 0.375
- w_key: bfloat16 [256, 256], replicated, may hold values from -0.375 to 0.375
- w_value: bfloat16 [256, 256], replicated, may hold values from -0.375 to 0.375
- lengths: int32 [128], P(('group', 'batch')), may hold values from 1 to 512, as said below
- item_rows: int32 [65536], P(('group', 'batch')), may hold values from 0 to 2047, as said below
- tile_owner: int32 [512], P(('group', 'batch')), may hold values from 0 to 3, as said below
Outputs:
- table_grad: float32 [8192, 256], P(('group', 'batch'))
Inputs may be any that keep to these rules, and one draw needn't show every extreme that they name: `lengths`: a history's live tokens are its first positions; in every draw some history has exactly 512 live tokens. `tile_owner`: among the first 8 tiles of each device's own tiles, and among the last 8, every group owns exactly 2 tiles. `item_rows`: of the 128 tokens of each tile, at most 32 have rows r with the same r // 256, and in every tile some value of r // 256 is taken by exactly 32 tokens.
All inputs are finite; a program needn't handle non-finite values.
Results may differ from a plain program's by a relative error of at most 0.0024.
The roundings to bfloat16 on the way count: a program that leaves them out, or rounds other values in their place, can miss the bound.
Values may be sent and summed in bfloat16 or wider, within the bound.
No kernel may reach another device: no remote copies, remote signals or barrier semaphores. Data moves between devices by JAX's collectives and lax.ppermute only.
A program may use at most 64 MiB of HBM per device.

v0:
```python
import math

import jax
import jax.numpy as jnp
from jax import lax
from jax.sharding import PartitionSpec as P

HEADS = 2
TILE = 128
SEQ_LEN = 512
ROWS_DEV = 256


def sequence_grads(query, key_rows, value, grad_out, count, w_query, w_key, w_value):
    span = query.shape[0]
    position = lax.broadcasted_iota(jnp.int32, (span, span), 0)
    other = lax.broadcasted_iota(jnp.int32, (span, span), 1)
    live = ((other <= position) & (position < count)).astype(jnp.float32)
    weight = live / count.astype(jnp.float32)
    scale = 1.0 / math.sqrt(query.shape[2])
    scores = jnp.einsum("ihd,jhd->hij", query, key_rows, preferred_element_type=jnp.float32) * scale
    sigma = jax.nn.sigmoid(scores)
    attend = (scores * sigma * weight).astype(jnp.bfloat16)
    value_grad = jnp.einsum(
        "hij,ihd->jhd", attend, grad_out, preferred_element_type=jnp.float32
    ).astype(jnp.bfloat16)
    attend_grad = jnp.einsum("ihd,jhd->hij", grad_out, value, preferred_element_type=jnp.float32)
    score_grad = (attend_grad * weight * sigma * (1.0 + scores * (1.0 - sigma))).astype(
        jnp.bfloat16
    )
    query_grad = (
        jnp.einsum("hij,jhd->ihd", score_grad, key_rows, preferred_element_type=jnp.float32) * scale
    ).astype(jnp.bfloat16)
    key_grad = (
        jnp.einsum("hij,ihd->jhd", score_grad, query, preferred_element_type=jnp.float32) * scale
    ).astype(jnp.bfloat16)
    width = w_query.shape[0]
    token = jnp.dot(query_grad.reshape(span, width), w_query.T, preferred_element_type=jnp.float32)
    token = token + jnp.dot(
        key_grad.reshape(span, width), w_key.T, preferred_element_type=jnp.float32
    )
    token = token + jnp.dot(
        value_grad.reshape(span, width), w_value.T, preferred_element_type=jnp.float32
    )
    return token.astype(jnp.bfloat16)


def token_grads(embeds, out_grad, w_query, w_key, w_value, lengths):
    history_count = lengths.shape[0]
    width = embeds.shape[1]
    head_size = width // HEADS

    def project(weight_matrix):
        return (
            jnp.dot(embeds, weight_matrix, preferred_element_type=jnp.float32)
            .astype(jnp.bfloat16)
            .reshape(history_count, SEQ_LEN, HEADS, head_size)
        )

    query = project(w_query)
    key_rows = project(w_key)
    value = project(w_value)
    grad_heads = out_grad.reshape(history_count, SEQ_LEN, HEADS, head_size)
    half_span = SEQ_LEN // 2

    def short_history(item):
        front = sequence_grads(
            item[0][:half_span],
            item[1][:half_span],
            item[2][:half_span],
            item[3][:half_span],
            item[4],
            w_query,
            w_key,
            w_value,
        )
        return jnp.concatenate(
            [front, jnp.zeros((SEQ_LEN - half_span, width), jnp.bfloat16)], axis=0
        )

    def whole_history(item):
        return sequence_grads(item[0], item[1], item[2], item[3], item[4], w_query, w_key, w_value)

    def one_history(item):
        return lax.cond(item[4] <= half_span, short_history, whole_history, item)

    result = lax.map(one_history, (query, key_rows, value, grad_heads, lengths))
    return result.reshape(history_count * SEQ_LEN, width)


def onehot_sum(row_count, tile_values, tile_rows, block_rows, initial):
    width = tile_values.shape[-1]
    flat_values = tile_values.reshape(-1, width)
    flat_rows = tile_rows.reshape(-1)
    step_count = flat_rows.shape[0] // block_rows
    target = lax.broadcasted_iota(jnp.int32, (row_count, 1), 0)

    def add_block(accum, item):
        onehot = (target == item[1][None, :]).astype(jnp.bfloat16)
        return (accum + jnp.dot(onehot, item[0], preferred_element_type=jnp.float32), None)

    blocks = (
        flat_values.reshape(step_count, block_rows, width),
        flat_rows.reshape(step_count, block_rows),
    )
    accum, unused = lax.scan(add_block, initial, blocks)
    return accum


def on_device(embeds, out_grad, w_query, w_key, w_value, lengths, item_rows, tile_owner):
    live_total = lax.psum(jnp.sum(lengths.astype(jnp.float32)), ("group", "batch"))
    device_count = lax.axis_size("group") * lax.axis_size("batch")
    scale_factor = embeds.shape[0] * device_count / live_total
    token_grad = token_grads(embeds, out_grad, w_query, w_key, w_value, lengths)
    width = token_grad.shape[1]
    ranking = jnp.argsort(tile_owner, stable=True)
    tile_values = token_grad.reshape(-1, TILE, width)[ranking]
    tile_rows = item_rows.reshape(-1, TILE)[ranking]
    got_values, got_rows = (
        lax.all_to_all(tile_values, "group", split_axis=0, concat_axis=0, tiled=True),
        lax.all_to_all(tile_rows, "group", split_axis=0, concat_axis=0, tiled=True),
    )
    empty_rows = jnp.zeros((ROWS_DEV * lax.axis_size("batch"), width), jnp.float32)
    table = lax.psum_scatter(
        onehot_sum(ROWS_DEV * lax.axis_size("batch"), got_values, got_rows, 4 * TILE, empty_rows),
        "batch",
        scatter_dimension=0,
        tiled=True,
    )
    return scale_factor * table


def solution(mesh):
    in_specs = (
        P(("group", "batch"), None),
        P(("group", "batch"), None),
        P(),
        P(),
        P(),
        P(("group", "batch")),
        P(("group", "batch")),
        P(("group", "batch")),
    )
    out_specs = P(("group", "batch"), None)
    return jax.shard_map(
        on_device, mesh=mesh, in_specs=in_specs, out_specs=out_specs, check_vma=False
    )
```

profile of v0, /device:TPU:0, one launch (start us, length us, event | category | flops | bytes accessed | tf_op | source)
XLA Modules:
  0.0 158.3 jit_solution(10579940593462021619)
XLA Ops:
  6.5 2.0 %sort.17 = (s32[16]{0:T(128)}, s32[16]{0:T(128)S(1)}) sort(s32[16]{0:T(128)} %param.21, s32[16]{0:T(128)S(1)} %iota.48), dimensions={0}, to_apply=%region_6.7 | sort | flops 64 | bytes 256 | tf_op jit(solution)/shard_map/jit(argsort)/sort | solution.py:116
  8.5 1.8 %gather_fusion = s32[16,128]{1,0:T(8,128)} fusion(s32[16,128]{1,0:T(8,128)} %bitcast.105, s32[1024]{0:T(1024)S(1)} %pad_clamp_fusion), kind=kCustom, calls=%fused_computation | custom fusion | bytes 16448 | tf_op jit(solution)/shard_map/gather | solution.py:118
  10.4 6.3 %all-to-all-start = ((s32[4,4,128]{2,1,0:T(4,128)}), s32[4,4,128]{2,1,0:T(4,128)S(1)}, u32[]{:S(2)}, u32[]{:S(2)}) async-start(s32[4,4,128]{2,1,0:T(4,128)} %bitcast.20), calls=%async_computation | async-start | bytes 16384 | tf_op jit(solution)/shard_map/all_to_all | solution.py:121
  16.7 2.2 %reshape.79 = bf16[4,512,2,128]{3,2,1,0:T(2,128)(2,1)} reshape(bf16[2048,256]{1,0:T(8,128)(2,1)} %param.15) | data formatting | bytes 2097152 | tf_op jit(solution)/shard_map/reshape | solution.py:63
  18.9 0.4 convolution_convert_fusion.4
  19.8 0.4 convolution_convert_fusion.3
  20.3 1.1 reshape.78
  21.4 0.4 convolution_convert_fusion.2
  21.8 1.1 reshape.80
  23.0 34.3 %while.21 = (s32[]{:T(128)}, bf16[4,512,256]{2,1,0:T(8,128)(2,1)}, s32[4]{0:T(128)S(1)}, bf16[4,512,2,128]{3,2,1,0:T(2,128)(2,1)S(1)}, bf16[4,512,2,128]{3,2,1,0...) while((s32[]{:T(128)}, bf16[4,512,256]{2,1,0:T(8,128)(2,1)}, ...), condition=%wide.region_5.6_spmd, body=%wide.region_2.5_spmd.sunk | while | flops 883687936 | bytes 23463240 | solution.py:87
  23.0 0.6 dynamic_slice.43
  24.3 1.4 constant_dynamic-slice_fusion.8
  25.8 1.3 constant_dynamic-slice_fusion.9
  27.2 3.6 %conditional.2 = (bf16[1,512,256]{2,1,0:T(8,128)(2,1)S(1)}) conditional(s32[]{:T(128)} %convert_element_type.105, (bf16[512,2,128]{2,0,1:T(8,128)(2,1)S(1)}, bf16[512,2,128]{2,0,1:T(8,128)(2,1)S(1)}, s32[]{:T(128)}, bf16[512,2,128]{2,0,1:T(8,128)(2,1)S(1)}, bf16[512,2,128]{2,0,1:T(8,128)(2,1)S(1)}, /*index=5*/bf16[256,256]{1,0:T(8,128)(2,1)S(1)}, ...), branch_computations={%region_3.3_spmd, %region_4.4_spmd} | conditional | flops 883687936 | bytes 18744356 | solution.py:85
  28.0 0.7 iota_compare_fusion.3
  29.3 0.3 convolution_convert_fusion.1
  30.8 0.7 constant_dynamic-update-slice_fusion.2
  31.6 0.6 dynamic_slice.43
  32.9 1.4 constant_dynamic-slice_fusion.8
  34.4 1.3 constant_dynamic-slice_fusion.9
  35.8 3.6 %conditional.2 = (bf16[1,512,256]{2,1,0:T(8,128)(2,1)S(1)}) conditional(s32[]{:T(128)} %convert_element_type.105, (bf16[512,2,128]{2,0,1:T(8,128)(2,1)S(1)}, bf16[512,2,128]{2,0,1:T(8,128)(2,1)S(1)}, s32[]{:T(128)}, bf16[512,2,128]{2,0,1:T(8,128)(2,1)S(1)}, bf16[512,2,128]{2,0,1:T(8,128)(2,1)S(1)}, /*index=5*/bf16[256,256]{1,0:T(8,128)(2,1)S(1)}, ...), branch_computations={%region_3.3_spmd, %region_4.4_spmd} | conditional | flops 883687936 | bytes 18744356 | solution.py:85
  36.5 0.7 iota_compare_fusion.3
  39.4 0.7 constant_dynamic-update-slice_fusion.2
  40.1 0.6 dynamic_slice.43
  41.5 1.4 constant_dynamic-slice_fusion.8
  43.0 1.3 constant_dynamic-slice_fusion.9
  44.4 3.6 %conditional.2 = (bf16[1,512,256]{2,1,0:T(8,128)(2,1)S(1)}) conditional(s32[]{:T(128)} %convert_element_type.105, (bf16[512,2,128]{2,0,1:T(8,128)(2,1)S(1)}, bf16[512,2,128]{2,0,1:T(8,128)(2,1)S(1)}, s32[]{:T(128)}, bf16[512,2,128]{2,0,1:T(8,128)(2,1)S(1)}, bf16[512,2,128]{2,0,1:T(8,128)(2,1)S(1)}, /*index=5*/bf16[256,256]{1,0:T(8,128)(2,1)S(1)}, ...), branch_computations={%region_3.3_spmd, %region_4.4_spmd} | conditional | flops 883687936 | bytes 18744356 | solution.py:85
  45.1 0.7 iota_compare_fusion.3
  48.0 0.7 constant_dynamic-update-slice_fusion.2
  48.7 0.6 dynamic_slice.43
  50.1 1.4 constant_dynamic-slice_fusion.8
  51.5 1.3 constant_dynamic-slice_fusion.9
  53.0 3.6 %conditional.2 = (bf16[1,512,256]{2,1,0:T(8,128)(2,1)S(1)}) conditional(s32[]{:T(128)} %convert_element_type.105, (bf16[512,2,128]{2,0,1:T(8,128)(2,1)S(1)}, bf16[512,2,128]{2,0,1:T(8,128)(2,1)S(1)}, s32[]{:T(128)}, bf16[512,2,128]{2,0,1:T(8,128)(2,1)S(1)}, bf16[512,2,128]{2,0,1:T(8,128)(2,1)S(1)}, /*index=5*/bf16[256,256]{1,0:T(8,128)(2,1)S(1)}, ...), branch_computations={%region_3.3_spmd, %region_4.4_spmd} | conditional | flops 883687936 | bytes 18744356 | solution.py:85
  53.7 0.7 iota_compare_fusion.3
  56.6 0.7 constant_dynamic-update-slice_fusion.2
  57.3 2.9 %gather_fusion.1 = bf16[16,128,256]{2,1,0:T(8,128)(2,1)} fusion(bf16[16,128,256]{2,1,0:T(8,128)(2,1)} %bitcast.104, s32[1024]{0:T(1024)S(1)} %pad_clamp_fusion), kind=kCustom, calls=%fused_computation.1 | custom fusion | bytes 2097216 | tf_op jit(solution)/shard_map/gather | solution.py:117
  60.2 5.1 %all-to-all-start.1 = ((bf16[16,128,256]{2,1,0:T(8,128)(2,1)}), bf16[16,128,256]{2,1,0:T(8,128)(2,1)}, u32[]{:S(2)}, u32[]{:S(2)}) async-start(bf16[16,128,256]{2,1,0:T(8,128)(2,1)} %gather_fusion.1), calls=%async_computation.1 | async-start | bytes 2097152 | tf_op jit(solution)/shard_map/all_to_all | solution.py:120
  65.3 25.3 %all-to-all-done.1 = bf16[16,128,256]{2,1,0:T(8,128)(2,1)} async-done(((bf16[16,128,256]{2,1,0:T(8,128)(2,1)}), bf16[16,128,256]{2,1,0:T(8,128)(2,1)}, u32[]{:S(2)}, u32[]{:S(2)}) %all-to-all-start.1) | async-done | bytes 1048608 | tf_op jit(solution)/shard_map/all_to_all | solution.py:120
  90.5 9.5 %while.22 = (s32[]{:T(128)}, f32[2048,256]{1,0:T(8,128)S(1)}, s32[4,512]{1,0:T(4,128)S(1)}, bf16[4,512,256]{2,1,0:T(8,128)(2,1)}, s32[]{:T(128)}, /*index=5*/s32[]{:T(128)}) while((s32[]{:T(128)}, f32[2048,256]{1,0:T(8,128)S(1)}, s32[4,512]{1,0:T(4,128)S(1)}, bf16[4,512,256]{2,1,0:T(8,128)(2,1)}, s32[]{:T(128)}, ...), condition=%wide.region_8.9_spmd.clone, body=%wide.region_7.8_spmd.clone.sunk | while | flops 538968064 | bytes 4462687 | solution.py:106
  90.5 2.3 %fusion.67 = f32[2048,256]{1,0:T(8,128)S(1)} fusion(f32[2048,256]{1,0:T(8,128)S(1)} %get-tuple-element.362, s32[512]{0:T(512)S(1)} %bitcast.106, pred[]{:T(512)S(6)} %compare.8, bf16[4,512,256]{2,1,0:T(8,128)(2,1)} %get-tuple-element.370, s32[]{:T(128)S(6)} %copy.74), kind=kOutput, calls=%fused_computation.60.clone.1 | convolution fusion | flops 538968064 | bytes 4458501 | tf_op jit(solution)/shard_map/while/body/eval_jaxpr/dot_general | solution.py:100
  92.9 2.3 %fusion.67 = f32[2048,256]{1,0:T(8,128)S(1)} fusion(f32[2048,256]{1,0:T(8,128)S(1)} %get-tuple-element.362, s32[512]{0:T(512)S(1)} %bitcast.106, pred[]{:T(512)S(6)} %compare.8, bf16[4,512,256]{2,1,0:T(8,128)(2,1)} %get-tuple-element.370, s32[]{:T(128)S(6)} %copy.74), kind=kOutput, calls=%fused_computation.60.clone.1 | convolution fusion | flops 538968064 | bytes 4458501 | tf_op jit(solution)/shard_map/while/body/eval_jaxpr/dot_general | solution.py:100
  95.3 2.3 %fusion.67 = f32[2048,256]{1,0:T(8,128)S(1)} fusion(f32[2048,256]{1,0:T(8,128)S(1)} %get-tuple-element.362, s32[512]{0:T(512)S(1)} %bitcast.106, pred[]{:T(512)S(6)} %compare.8, bf16[4,512,256]{2,1,0:T(8,128)(2,1)} %get-tuple-element.370, s32[]{:T(128)S(6)} %copy.74), kind=kOutput, calls=%fused_computation.60.clone.1 | convolution fusion | flops 538968064 | bytes 4458501 | tf_op jit(solution)/shard_map/while/body/eval_jaxpr/dot_general | solution.py:100
  97.7 2.3 %fusion.67 = f32[2048,256]{1,0:T(8,128)S(1)} fusion(f32[2048,256]{1,0:T(8,128)S(1)} %get-tuple-element.362, s32[512]{0:T(512)S(1)} %bitcast.106, pred[]{:T(512)S(6)} %compare.8, bf16[4,512,256]{2,1,0:T(8,128)(2,1)} %get-tuple-element.370, s32[]{:T(128)S(6)} %copy.74), kind=kOutput, calls=%fused_computation.60.clone.1 | convolution fusion | flops 538968064 | bytes 4458501 | tf_op jit(solution)/shard_map/while/body/eval_jaxpr/dot_general | solution.py:100
  100.0 1.3 copy-done.1
  101.4 0.6 convert_reduce_fusion
  102.0 45.7 %psum.7 = f32[]{:T(128)} all-reduce(f32[]{:T(128)} %convert_reduce_fusion), channel_id=1, replica_groups=mesh['group'=4,'batch'=8] {'group','batch'}, use_global_device_ids=true, to_apply=%region_1.0 | all-reduce | flops 1 | bytes 8 | tf_op jit(solution)/shard_map/psum | solution.py:111
  148.4 1.4 reduce-scatter.2.cloned.1.call-done
  149.8 1.7 %broadcast_multiply_fusion = f32[256,256]{1,0:T(8,128)} fusion(f32[256,256]{1,0:T(8,128)} %reduce-scatter.2.cloned.1.call-done, f32[]{:T(128)S(6)} %div.21), kind=kLoop, calls=%fused_computation.69 | loop fusion | flops 65536 | bytes 524292 | tf_op jit(solution)/shard_map/mul | solution.py:130
  (80 shorter events, 9.3 us)
Async XLA Ops:
  6.5 12.4 %copy-start = (bf16[2048,256]{1,0:T(8,128)(2,1)S(1)}, bf16[2048,256]{1,0:T(8,128)(2,1)}, u32[]{:S(2)}) copy-start(bf16[2048,256]{1,0:T(8,128)(2,1)} %param.14) | copy-start | bytes 3145732
  6.5 12.4 %copy-start.3 = (bf16[256,256]{1,0:T(8,128)(2,1)S(1)}, bf16[256,256]{1,0:T(8,128)(2,1)}, u32[]{:S(2)}) copy-start(bf16[256,256]{1,0:T(8,128)(2,1)} %param.16) | copy-start | bytes 393220
  10.4 49.8 %all-to-all-start = ((s32[4,4,128]{2,1,0:T(4,128)}), s32[4,4,128]{2,1,0:T(4,128)S(1)}, u32[]{:S(2)}, u32[]{:S(2)}) async-start(s32[4,4,128]{2,1,0:T(4,128)} %bitcast.20), calls=%async_computation | async-start | bytes 16384 | tf_op jit(solution)/shard_map/all_to_all | solution.py:121
  18.9 0.9 copy-start.4
  19.8 1.6 copy-start.2
  21.4 1.6 %copy-start.5 = (s32[4]{0:T(128)S(1)}, s32[4]{0:T(128)}, u32[]{:S(2)}) copy-start(s32[4]{0:T(128)} %param.19) | copy-start | bytes 52
  60.2 30.4 %all-to-all-start.1 = ((bf16[16,128,256]{2,1,0:T(8,128)(2,1)}), bf16[16,128,256]{2,1,0:T(8,128)(2,1)}, u32[]{:S(2)}, u32[]{:S(2)}) async-start(bf16[16,128,256]{2,1,0:T(8,128)(2,1)} %gather_fusion.1), calls=%async_computation.1 | async-start | bytes 2097152 | tf_op jit(solution)/shard_map/all_to_all | solution.py:120
  65.3 84.6 %reduce-scatter.2.cloned.1.call-start = ((), (), s32[]{:S(2)}) async-start(), calls=%async_computation.3 | async-start | bytes 2359296 | tf_op jit(solution)/shard_map/reduce_scatter | solution.py:124
  100.0 1.3 copy-start.1
Sparse Core Ops, SparseCore 0:
  101.5 48.2 reduce-scatter.1
where the time goes:
time: 159 us; the launch traced here: 158 us
  blocking collectives  45.7 us (29%)
  local copies, waits for them, and re-layouts  28 us (18%)
  waiting for transfers between devices  26.7 us (17%)
  matrix products  18.7 us (12%)
  between operations  14.1 us (9%)
  starting transfers between devices  11.4 us (7%)
  other arithmetic  7.41 us (5%)
  loops' own time  6.25 us (4%)
    psum x1, blocking collectives, on_device(): lax.psum(jnp.sum(lengths.astype(jnp.float32)), ('group', 'batch'))  45.7 us
    all_to_all x1, waiting for transfers between devices, on_device(): lax.all_to_all(tile_values, 'group', split_axis=0, concat_axis=0, tiled=T...  25.3 us
    dynamic_slice x28, local copies, waits for them, and re-layouts, token_grads(): result = lax.map(one_history, (query, key_rows, value, grad_heads, lengths))  14 us
    dot_general x4, matrix products, add_block(): jnp.dot(onehot, item[0], preferred_element_type=jnp.float32)  9.34 us
    all_to_all x1, starting transfers between devices, on_device(): lax.all_to_all(tile_rows, 'group', split_axis=0, concat_axis=0, tiled=True)  6.35 us
    all_to_all x1, starting transfers between devices, on_device(): lax.all_to_all(tile_values, 'group', split_axis=0, concat_axis=0, tiled=T...  5.09 us
    another operation x4, loops' own time, one_history(): return lax.cond(item[4] <= half_span, short_history, whole_history, item)  3.22 us
  transfers between devices with their start and end apart: 3, of which 2 were waited for; matrix products, arithmetic and copies ran while one was open for 24% of the time, Pallas kernels for 0%

commit v1 on v0

v1 whole, which is shorter than its diff:
```python
import functools
import math

import jax
import jax.numpy as jnp
from jax import lax
from jax.experimental import pallas as pl
from jax.experimental.pallas import tpu as pltpu
from jax.sharding import PartitionSpec as P

HEADS = 2
ROWS_DEV = 256
EXTRA = 16
BASE = 128
NT = (((1,), (1,)), ((), ()))
TN = (((0,), (0,)), ((), ()))


def dot(a, b, dims=(((1,), (0,)), ((), ()))):
    return lax.dot_general(a, b, dims, preferred_element_type=jnp.float32)


def digits_row(total, width):
    lane = lax.broadcasted_iota(jnp.int32, (1, width), 1)
    low, mid, high = total % BASE, (total // BASE) % BASE, total // (BASE * BASE)
    row = jnp.where(lane == 0, low, jnp.where(lane == 1, mid, jnp.where(lane == 2, high, 0)))
    return row.astype(jnp.float32)


def total_of_digits(row):
    return row[:, 0:1] + row[:, 1:2] * float(BASE) + row[:, 2:3] * float(BASE * BASE)


def attention_kernel(
    half, half_seqs, half_tiles, groups, tile, extra,
    len_ref, own_ref, emb, gout, wq, wk, wv, rows, *refs,
):
    outs = refs[:groups]
    q_s, k_s, v_s, dq_s, dk_s, dv_s, tok_s, ext_s, idx_s = refs[groups:]
    step = pl.program_id(0)
    span, width = emb.shape
    head = width // HEADS
    scale = 1.0 / math.sqrt(head)
    count = len_ref[half * half_seqs + step]
    block = span // 2

    def gate(raw, grad, weight):
        grown = jnp.exp(raw * (-scale))
        sigma = 1.0 / (1.0 + grown)
        act = raw * scale * sigma
        slope = sigma + act * (1.0 - sigma)
        return (
            (act * weight).astype(jnp.bfloat16),
            (grad * weight * slope).astype(jnp.bfloat16),
        )

    def run(live):
        base = pl.multiple_of(step * span, span)
        q_s[0:live, :] = dot(emb[0:live, :], wq[...]).astype(jnp.bfloat16)
        k_s[0:live, :] = dot(emb[0:live, :], wk[...]).astype(jnp.bfloat16)
        v_s[0:live, :] = dot(emb[0:live, :], wv[...]).astype(jnp.bfloat16)
        lane = lax.broadcasted_iota(jnp.int32, (1, block), 1)
        inverse = 1.0 / jnp.broadcast_to(count, (1, block)).astype(jnp.float32)
        sub = lax.broadcasted_iota(jnp.int32, (block, block), 0)
        lan = lax.broadcasted_iota(jnp.int32, (block, block), 1)
        causal = sub <= lan
        for h in range(HEADS):
            cols = slice(h * head, (h + 1) * head)
            att, sco = {}, {}
            for i in range(live // block):
                weight = jnp.where(lane + i * block < count, inverse, 0.0)
                iq = q_s[i * block:(i + 1) * block, cols]
                ig = gout[i * block:(i + 1) * block, cols]
                for j in range(i + 1):
                    jk = k_s[j * block:(j + 1) * block, cols]
                    jv = v_s[j * block:(j + 1) * block, cols]
                    raw = dot(jk, iq, NT)
                    grad = dot(jv, ig, NT)
                    if i == j:
                        use = jnp.where(causal, weight, 0.0)
                    else:
                        use = weight
                    att[j, i], sco[j, i] = gate(raw, grad, use)
            for j in range(live // block):
                vg = kg = None
                for i in range(j, live // block):
                    iq = q_s[i * block:(i + 1) * block, cols]
                    ig = gout[i * block:(i + 1) * block, cols]
                    a, b = dot(att[j, i], ig), dot(sco[j, i], iq)
                    vg = a if vg is None else vg + a
                    kg = b if kg is None else kg + b
                dv_s[j * block:(j + 1) * block, cols] = vg.astype(jnp.bfloat16)
                dk_s[j * block:(j + 1) * block, cols] = (kg * scale).astype(jnp.bfloat16)
            for i in range(live // block):
                qg = None
                for j in range(i + 1):
                    jk = k_s[j * block:(j + 1) * block, cols]
                    c = dot(sco[j, i], jk, TN)
                    qg = c if qg is None else qg + c
                dq_s[i * block:(i + 1) * block, cols] = (qg * scale).astype(jnp.bfloat16)
        token = dot(dq_s[0:live, :], wq[...], NT)
        token = token + dot(dk_s[0:live, :], wk[...], NT)
        token = token + dot(dv_s[0:live, :], wv[...], NT)
        tok_s[pl.ds(base, live), :] = token.astype(jnp.bfloat16)
        if live < span:
            tok_s[pl.ds(base + live, span - live), :] = jnp.zeros(
                (span - live, width), jnp.bfloat16
            )

    @pl.when(count <= block)
    def _():
        run(block)

    @pl.when(count > block)
    def _():
        run(span)

    @pl.when(step == pl.num_programs(0) - 1)
    def _():
        me = lax.axis_index("group")
        owned = half_tiles // groups
        halves = own_ref.shape[0] // half_tiles

        def place(part):
            for g in range(groups):
                idx_s[groups * owned + g] = 0
            for t in range(half_tiles):
                owner = own_ref[part * half_tiles + t]
                seen = idx_s[groups * owned + owner]
                idx_s[owner * owned + seen] = t
                idx_s[groups * owned + owner] = seen + 1

        if extra:
            total = len_ref[0]
            for s in range(1, len_ref.shape[0]):
                total = total + len_ref[s]
            for k in range(groups):
                ext_s[k] = jnp.zeros(ext_s.shape[1:], jnp.float32)
                ext_s[k, halves * owned:halves * owned + 1, :] = digits_row(total, width)
            for part in range(halves):
                place(part)
                for k in range(groups):
                    owner = me ^ k
                    for s in range(owned):
                        t = idx_s[owner * owned + s] + part * half_tiles
                        row = rows[pl.ds(t, 1), :]
                        at = part * owned + s
                        ext_s[k, at:at + 1, 0:tile] = (row // ROWS_DEV).astype(jnp.float32)
                        ext_s[k, at:at + 1, tile:2 * tile] = (row % ROWS_DEV).astype(jnp.float32)
            for k in range(groups):
                outs[k][owned * tile:owned * tile + EXTRA, :] = ext_s[k].astype(jnp.bfloat16)
        place(half)
        for k in range(groups):
            owner = me ^ k
            for s in range(owned):
                t = idx_s[owner * owned + s]
                outs[k][s * tile:(s + 1) * tile, :] = tok_s[
                    pl.ds(pl.multiple_of(t * tile, tile), tile), :
                ]


def attention(half, halves, groups, lengths, owners, embeds, out_grad, wq, wk, wv, rows, extra):
    tokens, width = embeds.shape
    seqs = lengths.shape[0]
    span = tokens // seqs
    tile = tokens // owners.shape[0]
    half_seqs, half_tiles = seqs // halves, owners.shape[0] // halves
    owned = half_tiles // groups
    out_rows = owned * tile + (EXTRA if extra else 0)
    whole = lambda s: (0, 0)
    smem = pl.BlockSpec(memory_space=pltpu.SMEM)
    flops = half_seqs * (2 * span * width * width * 6 + 10 * span * span * width)
    return pl.pallas_call(
        functools.partial(attention_kernel, half, half_seqs, half_tiles, groups, tile, extra),
        grid=(half_seqs,),
        in_specs=[
            smem, smem,
            pl.BlockSpec((span, width), lambda s: (half * half_seqs + s, 0)),
            pl.BlockSpec((span, width), lambda s: (half * half_seqs + s, 0)),
            pl.BlockSpec((width, width), whole),
            pl.BlockSpec((width, width), whole),
            pl.BlockSpec((width, width), whole),
            pl.BlockSpec((owners.shape[0], tile), whole),
        ],
        out_specs=[pl.BlockSpec((out_rows, width), whole)] * groups,
        out_shape=[jax.ShapeDtypeStruct((out_rows, width), jnp.bfloat16)] * groups,
        scratch_shapes=[pltpu.VMEM((span, width), jnp.bfloat16)] * 6 + [
            pltpu.VMEM((half_seqs * span, width), jnp.bfloat16),
            pltpu.VMEM((groups, EXTRA, width), jnp.float32),
            pltpu.SMEM((groups * owned + groups,), jnp.int32),
        ],
        cost_estimate=pl.CostEstimate(
            flops=flops, bytes_accessed=4 * half_seqs * span * width * 2, transcendentals=0
        ),
        name=f"attention_{half}",
    )(lengths, owners, embeds, out_grad, wq, wk, wv, rows)


def keys_of(ext, slots, tile):
    high = jnp.concatenate([e[s:s + 1, 0:tile] for e, s in slots], axis=1)
    low = jnp.concatenate([e[s:s + 1, tile:2 * tile] for e, s in slots], axis=1)
    return high, low


def sums_of(block, boxes, exts, first, owned, tile):
    total = None
    row = lax.broadcasted_iota(jnp.int32, (ROWS_DEV, owned * tile), 0).astype(jnp.float32)
    for box, ext in zip(boxes, exts):
        high = jnp.concatenate(
            [ext[first + s:first + s + 1, 0:tile] for s in range(owned)], axis=1
        ).astype(jnp.float32)
        low = jnp.concatenate(
            [ext[first + s:first + s + 1, tile:2 * tile] for s in range(owned)], axis=1
        ).astype(jnp.float32)
        key = jnp.where(high == block.astype(jnp.float32), low, -1.0)
        hot = jnp.where(row == key, 1.0, 0.0).astype(jnp.bfloat16)
        part = dot(hot, box[0:owned * tile, :])
        total = part if total is None else total + part
    return total


def first_kernel(pairs, owned, tile, *refs):
    boxes, acc = refs[:-1], refs[-1]
    core = lax.axis_index("batch") % 2
    base = owned * tile
    exts = [b[base:base + EXTRA, :] for b in boxes]
    for side in range(2):
        for p in range(pairs):
            block = 2 * p + (1 - core if side == 0 else core)
            acc[side, p] = sums_of(block, boxes, exts, 0, owned, tile)


def live_of(exts, at):
    total = None
    for e in exts:
        row = total_of_digits(e[at:at + 1, :].astype(jnp.float32))
        total = row if total is None else total + row
    return total


def digits_of_float(total, width):
    return digits_row(jnp.broadcast_to(total, (1, width)).astype(jnp.int32), width)


def second_kernel(side, pairs, owned, tile, groups, *refs):
    boxes, firsts, acc, out = refs[:groups], refs[groups:2 * groups], refs[-2], refs[-1]
    core = lax.axis_index("batch") % 2
    base = owned * tile
    exts = [b[base:base + EXTRA, :] for b in firsts]
    width = out.shape[-1]
    for p in range(pairs):
        block = 2 * p + (1 - core if side == 0 else core)
        total = acc[0, p] + sums_of(block, boxes, exts, owned, owned, tile)
        out[p * ROWS_DEV:(p + 1) * ROWS_DEV, :] = total.astype(out.dtype)
    if side == 0:
        live = live_of(exts, 2 * owned)
        row = digits_of_float(live, width)
        out[pairs * ROWS_DEV:pairs * ROWS_DEV + EXTRA, :] = jnp.broadcast_to(
            row, (EXTRA, width)
        ).astype(out.dtype)


def pair_kernel(pairs, owned, tile, groups, *refs):
    firsts, own, got = refs[:groups], refs[groups], refs[groups + 1]
    outs = refs[groups + 2:]
    pair = lax.axis_index("batch") // 2
    base = owned * tile
    width = own.shape[-1]
    live = live_of([b[base:base + EXTRA, :] for b in firsts], 2 * owned)
    other = total_of_digits(got[pairs * ROWS_DEV:pairs * ROWS_DEV + 1, :].astype(jnp.float32))
    both = digits_of_float(live + other, width)
    for k in range(pairs):
        at = pl.multiple_of((pair ^ k) * ROWS_DEV, ROWS_DEV)
        total = own[pl.ds(at, ROWS_DEV), :] + got[pl.ds(at, ROWS_DEV), :].astype(jnp.float32)
        outs[k][0:ROWS_DEV, :] = total.astype(outs[k].dtype)
        outs[k][ROWS_DEV:ROWS_DEV + EXTRA, :] = jnp.broadcast_to(both, (EXTRA, width)).astype(
            outs[k].dtype
        )


def last_kernel(tokens_all, *refs):
    ins, out = refs[:-1], refs[-1]
    total = live = None
    for r in ins:
        part = r[0:ROWS_DEV, :].astype(jnp.float32)
        some = total_of_digits(r[ROWS_DEV:ROWS_DEV + 1, :].astype(jnp.float32))
        total = part if total is None else total + part
        live = some if live is None else live + some
    out[...] = total * (tokens_all / live)


def vmem(n):
    return [pl.BlockSpec(memory_space=pltpu.VMEM)] * n


def on_device(groups, batches, embeds, out_grad, w_query, w_key, w_value, lengths, item_rows,
              tile_owner):
    tokens, width = embeds.shape
    halves = 2
    tile = tokens // tile_owner.shape[0]
    owned = tile_owner.shape[0] // halves // groups
    pairs = batches // 2
    rows = item_rows.reshape(-1, tile)
    f32, bf16 = jnp.float32, jnp.bfloat16

    def swap(box, k):
        return lax.ppermute(box, "group", [(i, i ^ k) for i in range(groups)])

    boxes = []
    for half in range(halves):
        mine = attention(
            half, halves, groups, lengths, tile_owner, embeds, out_grad,
            w_query, w_key, w_value, rows, half == 0,
        )
        boxes.append([mine[0]] + [swap(mine[k], k) for k in range(1, groups)])

    def call(kernel, shapes, name, flops, *args):
        return pl.pallas_call(
            kernel,
            in_specs=vmem(len(args)),
            out_specs=vmem(len(shapes)) if isinstance(shapes, list) else vmem(1)[0],
            out_shape=shapes,
            cost_estimate=pl.CostEstimate(flops=flops, bytes_accessed=1 << 20, transcendentals=0),
            name=name,
        )(*args)

    shape = jax.ShapeDtypeStruct
    work = 2 * pairs * ROWS_DEV * width * owned * tile * groups
    acc = call(
        functools.partial(first_kernel, pairs, owned, tile),
        shape((2, pairs, ROWS_DEV, width), f32), "sums_first", 2 * work, *boxes[0],
    )

    def second(side, out):
        return pl.pallas_call(
            functools.partial(second_kernel, side, pairs, owned, tile, groups),
            grid=(1,),
            in_specs=vmem(2 * groups) + [
                pl.BlockSpec((1, pairs, ROWS_DEV, width), lambda s: (side, 0, 0, 0))
            ],
            out_specs=vmem(1)[0],
            out_shape=out,
            cost_estimate=pl.CostEstimate(
                flops=work, bytes_accessed=1 << 20, transcendentals=0
            ),
            name=f"sums_second_{side}",
        )(*boxes[1], *boxes[0], acc)

    send = second(0, shape((pairs * ROWS_DEV + EXTRA, width), bf16))
    got = lax.ppermute(send, "batch", [(i, i ^ 1) for i in range(batches)])
    own = second(1, shape((pairs * ROWS_DEV, width), f32))
    parts = call(
        functools.partial(pair_kernel, pairs, owned, tile, groups),
        [shape((ROWS_DEV + EXTRA, width), f32 if k == 0 else bf16) for k in range(pairs)],
        "pair_sums", 1 << 22, *boxes[0], own, got,
    )
    ends = [parts[0]] + [
        lax.ppermute(parts[k], "batch", [(i, i ^ (2 * k)) for i in range(batches)])
        for k in range(1, pairs)
    ]
    tokens_all = float(tokens * groups * batches)
    return call(
        functools.partial(last_kernel, tokens_all),
        shape((ROWS_DEV, width), f32), "final", 1 << 20, *ends,
    )


def solution(mesh):
    groups, batches = mesh.shape["group"], mesh.shape["batch"]
    both = P(("group", "batch"))
    wide = P(("group", "batch"), None)
    return jax.shard_map(
        functools.partial(on_device, groups, batches),
        mesh=mesh,
        in_specs=(wide, wide, P(), P(), P(), both, both, both),
        out_specs=wide,
        check_vma=False,
    )
```

time: 159 us -> 58.8 us (0.37)
  blocking collectives: 45.7 us -> 0 us
  local copies, waits for them, and re-layouts: 28 us -> 2.88 us
  Pallas kernels: 0 us -> 24.4 us
  matrix products: 18.7 us -> 0 us
  between operations: 14.1 us -> 0.03 us
  waiting for transfers between devices: 26.7 us -> 16.2 us
  other arithmetic: 7.41 us -> 0 us
  loops' own time: 6.25 us -> 0 us
  starting transfers between devices: 11.4 us -> 15 us
    psum x1 -> x0, blocking collectives: 45.7 us -> none  [on_device(): lax.psum(jnp.sum(lengths.astype(jnp.float32)), ('group', 'batch'))]
    all_to_all x2 -> x0, waiting for transfers between devices: 25.3 us -> none  [the longest x1 25.3 us: on_device(): lax.all_to_all(tile_values, 'group', split_axis=0, concat_axis=0, tiled=T...]
    pallas_call x0 -> x7, Pallas kernels: none -> 24.4 us  [the longest x2 9.52 us: attention(): pl.pallas_call(functools.partial(attention_kernel, half, half_seqs, half_...]
    dot_general x39 -> x0, matrix products: 18.7 us -> none  [the longest x4 9.34 us: add_block(): jnp.dot(onehot, item[0], preferred_element_type=jnp.float32)]
    ppermute x0 -> x10, waiting for transfers between devices: none -> 16.2 us  [the longest x6 8.98 us: swap(): return lax.ppermute(box, 'group', [(i, i ^ k) for i in range(groups)])]
    ppermute x0 -> x10, starting transfers between devices: none -> 15 us  [the longest x6 10.1 us: swap(): return lax.ppermute(box, 'group', [(i, i ^ k) for i in range(groups)])]
    dynamic_slice x32 -> x0, local copies, waits for them, and re-layouts: 14.1 us -> none  [the longest x28 14 us: token_grads(): result = lax.map(one_history, (query, key_rows, value, grad_heads, lengths))]
    all_to_all x2 -> x0, starting transfers between devices: 11.4 us -> none  [the longest x1 6.35 us: on_device(): lax.all_to_all(tile_rows, 'group', split_axis=0, concat_axis=0, tiled=True)]
  transfers between devices with their start and end apart: 3 -> 10, of which waited for: 2 -> 4; matrix products, arithmetic and copies ran while one was open for 24% -> 0% of each run, Pallas kernels for 0% -> 20%
where the time goes in v1:
time: 58.8 us; the launch traced here: 58.6 us
  Pallas kernels  24.4 us (41%)
  waiting for transfers between devices  16.2 us (28%)
  starting transfers between devices  15 us (26%)
  local copies, waits for them, and re-layouts  2.88 us (5%)
    ppermute x6, starting transfers between devices, swap(): return lax.ppermute(box, 'group', [(i, i ^ k) for i in range(groups)])  10.1 us
    pallas_call x2, Pallas kernels, attention(): pl.pallas_call(functools.partial(attention_kernel, half, half_seqs, half_...  9.52 us
    ppermute x6, waiting for transfers between devices, swap(): return lax.ppermute(box, 'group', [(i, i ^ k) for i in range(groups)])  8.98 us
    pallas_call x3, Pallas kernels, call(): pl.pallas_call(kernel, in_specs=vmem(len(args)), out_specs=vmem(len(shape...  8.38 us
    ppermute x3, waiting for transfers between devices, on_device(): lax.ppermute(parts[k], 'batch', [(i, i ^ 2 * k) for i in range(batches)])  7.25 us
    pallas_call x2, Pallas kernels, second(): pl.pallas_call(functools.partial(second_kernel, side, pairs, owned, tile,...  6.53 us
    ppermute x3, starting transfers between devices, on_device(): lax.ppermute(parts[k], 'batch', [(i, i ^ 2 * k) for i in range(batches)])  4.92 us
    unnamed x20, local copies, waits for them, and re-layouts  2.88 us
  transfers between devices with their start and end apart: 10, of which 4 were waited for; matrix products, arithmetic and copies ran while one was open for 0% of the time, Pallas kernels for 20%

profile of v1, /device:TPU:0, one launch (start us, length us, event | category | flops | bytes accessed | tf_op | source)
XLA Modules:
  0.0 58.6 jit_solution(215325667877917604)
XLA Ops:
  0.0 4.8 %attention_0.1 = (bf16[272,256]{1,0:T(8,128)(2,1)}, bf16[272,256]{1,0:T(8,128)(2,1)}, bf16[272,256]{1,0:T(8,128)(2,1)}, bf16[272,256]{1,0:T(8,128)(2,1)}) custom-call(s32[4]{0:T(128)} %len_ref.3, s32[16]{0:T(128)} %own_ref.3, bf16[2048,256]{1,0:T(8,128)(2,1)} %emb.3, bf16[2048,256]{1,0:T(8,128)(2,1)} %gout.3, bf16[256,256]{1,0:T(8,128)(2,1)} %wq.3, ...), custom_call_target="tpu_custom_call" | custom-call | flops 2147483648 | bytes 2097152 | tf_op jit(solution)/shard_map/attention_0/pallas_call | solution.py:173
  4.8 3.1 %collective-permute-start = (bf16[272,256]{1,0:T(8,128)(2,1)}, bf16[272,256]{1,0:T(8,128)(2,1)S(1)}, u32[]{:S(2)}, u32[]{:S(2)}) collective-permute-start(bf16[272,256]{1,0:T(8,128)(2,1)} %get-tuple-element.18), channel_id=1, source_target_pairs={{0,8},{8,0},{16,24},{24,16},{1,9},{9,1},{17,25},{25,17},{2,10},{10... | collective-permute-start | bytes 417800 | tf_op jit(solution)/shard_map/ppermute | solution.py:307
  7.9 2.6 %collective-permute-start.1 = (bf16[272,256]{1,0:T(8,128)(2,1)}, bf16[272,256]{1,0:T(8,128)(2,1)S(1)}, u32[]{:S(2)}, u32[]{:S(2)}) collective-permute-start(bf16[272,256]{1,0:T(8,128)(2,1)} %get-tuple-element.19), channel_id=1, source_target_pairs={{0,16},{8,24},{16,0},{24,8},{1,17},{9,25},{17,1},{25,9},{2,18},{10... | collective-permute-start | bytes 417800 | tf_op jit(solution)/shard_map/ppermute | solution.py:307
  10.5 0.0 collective-permute-start.2
  10.5 4.7 %attention_1.1 = (bf16[256,256]{1,0:T(8,128)(2,1)}, bf16[256,256]{1,0:T(8,128)(2,1)}, bf16[256,256]{1,0:T(8,128)(2,1)}, bf16[256,256]{1,0:T(8,128)(2,1)}) custom-call(s32[4]{0:T(128)} %len_ref.3, s32[16]{0:T(128)} %own_ref.3, bf16[2048,256]{1,0:T(8,128)(2,1)} %emb.3, bf16[2048,256]{1,0:T(8,128)(2,1)} %gout.3, bf16[256,256]{1,0:T(8,128)(2,1)} %wq.3, ...), custom_call_target="tpu_custom_call" | custom-call | flops 2147483648 | bytes 2097152 | tf_op jit(solution)/shard_map/attention_1/pallas_call | solution.py:173
  15.2 0.9 %collective-permute-start.3 = (bf16[256,256]{1,0:T(8,128)(2,1)}, bf16[256,256]{1,0:T(8,128)(2,1)S(1)}, u32[]{:S(2)}, u32[]{:S(2)}) collective-permute-start(bf16[256,256]{1,0:T(8,128)(2,1)} %get-tuple-element.22), channel_id=1, source_target_pairs={{0,8},{8,0},{16,24},{24,16},{1,9},{9,1},{17,25},{25,17},{2,10},{10... | collective-permute-start | bytes 393224 | tf_op jit(solution)/shard_map/ppermute | solution.py:307
  16.1 3.5 %collective-permute-start.4 = (bf16[256,256]{1,0:T(8,128)(2,1)}, bf16[256,256]{1,0:T(8,128)(2,1)S(1)}, u32[]{:S(2)}, u32[]{:S(2)}) collective-permute-start(bf16[256,256]{1,0:T(8,128)(2,1)} %get-tuple-element.23), channel_id=1, source_target_pairs={{0,16},{8,24},{16,0},{24,8},{1,17},{9,25},{17,1},{25,9},{2,18},{10... | collective-permute-start | bytes 393224 | tf_op jit(solution)/shard_map/ppermute | solution.py:307
  19.6 0.0 collective-permute-done.refs_1_.refs_5_
  19.6 0.0 copy-start
  19.6 0.0 collective-permute-start.5
  19.6 2.0 %collective-permute-done.1.refs_2_.refs_6_ = bf16[272,256]{1,0:T(8,128)(2,1)S(1)} collective-permute-done((bf16[272,256]{1,0:T(8,128)(2,1)}, bf16[272,256]{1,0:T(8,128)(2,1)S(1)}, u32[]{:S(2)}, u32[]{:S(2)}) %collective-permute-start.1) | collective-permute-done | bytes 139296 | tf_op jit(solution)/shard_map/ppermute | solution.py:307
  21.5 0.0 copy-start.1
  21.5 0.0 collective-permute-done.2.refs_3_.refs_7_
  21.5 0.0 copy-start.2
  21.5 0.0 copy-done
  21.5 0.6 %copy-done.1 = bf16[272,256]{1,0:T(8,128)(2,1)} copy-done((bf16[272,256]{1,0:T(8,128)(2,1)}, bf16[272,256]{1,0:T(8,128)(2,1)S(1)}, u32[]{:S(2)}) %copy-start.1) | copy-done | bytes 139288
  22.2 0.0 copy-done.2
  22.2 3.7 %sums_first.1.refs_8_ = f32[2,4,256,256]{3,2,1,0:T(8,128)} custom-call(bf16[272,256]{1,0:T(8,128)(2,1)} %get-tuple-element.17.refs_0_.refs_4_, bf16[272,256]{1,0:T(8,128)(2,1)} %copy-done, bf16[272,256]{1,0:T(8,128)(2,1)} %copy-done.1, bf16[272,256]{1,0:T(8,128)(2,1)} %copy-done.2), custom_call_target="tpu_custom_call" | custom-call | flops 1073741824 | bytes 1048576 | tf_op jit(solution)/shard_map/sums_first/pallas_call | solution.py:318
  25.9 0.0 collective-permute-done.3.refs_1_
  25.9 0.0 copy-start.4
  25.9 7.0 %collective-permute-done.4.refs_2_ = bf16[256,256]{1,0:T(8,128)(2,1)S(1)} collective-permute-done((bf16[256,256]{1,0:T(8,128)(2,1)}, bf16[256,256]{1,0:T(8,128)(2,1)S(1)}, u32[]{:S(2)}, u32[]{:S(2)}) %collective-permute-start.4) | collective-permute-done | bytes 131104 | tf_op jit(solution)/shard_map/ppermute | solution.py:307
  32.9 0.0 copy-start.5
  32.9 0.0 collective-permute-done.5.refs_3_
  32.9 0.0 copy-start.6
  33.0 0.0 copy-done.4
  33.0 0.6 %copy-done.5 = bf16[256,256]{1,0:T(8,128)(2,1)} copy-done((bf16[256,256]{1,0:T(8,128)(2,1)}, bf16[256,256]{1,0:T(8,128)(2,1)S(1)}, u32[]{:S(2)}) %copy-start.5) | copy-done | bytes 131096
  33.6 0.0 copy-done.6
  33.6 3.2 %sums_second_0.1 = bf16[1040,256]{1,0:T(8,128)(2,1)} custom-call(bf16[256,256]{1,0:T(8,128)(2,1)} %get-tuple-element.21.refs_0_, bf16[256,256]{1,0:T(8,128)(2,1)} %copy-done.4, bf16[256,256]{1,0:T(8,128)(2,1)} %copy-done.5, bf16[256,256]{1,0:T(8,128)(2,1)} %copy-done.6, bf16[272,256]{1,0:T(8,128)(2,1)} %get-tuple-element.17.refs_0_.refs_4_, ...), custom_call_target="tpu_custom_call" | custom-call | flops 536870912 | bytes 1048576 | tf_op jit(solution)/shard_map/sums_second_0/pallas_call | solution.py:335
  36.8 0.0 collective-permute-start.6
  36.8 3.4 %sums_second_1.1.refs_4_ = f32[1024,256]{1,0:T(8,128)} custom-call(bf16[256,256]{1,0:T(8,128)(2,1)} %get-tuple-element.21.refs_0_, bf16[256,256]{1,0:T(8,128)(2,1)} %copy-done.4, bf16[256,256]{1,0:T(8,128)(2,1)} %copy-done.5, bf16[256,256]{1,0:T(8,128)(2,1)} %copy-done.6, bf16[272,256]{1,0:T(8,128)(2,1)} %get-tuple-element.17.refs_0_.refs_4_, ...), custom_call_target="tpu_custom_call" | custom-call | flops 536870912 | bytes 1048576 | tf_op jit(solution)/shard_map/sums_second_1/pallas_call | solution.py:335
  40.2 0.0 collective-permute-done.6.refs_5_
  40.2 0.0 copy-start.3
  40.2 0.8 %copy-done.3 = bf16[1040,256]{1,0:T(8,128)(2,1)} copy-done((bf16[1040,256]{1,0:T(8,128)(2,1)}, bf16[1040,256]{1,0:T(8,128)(2,1)S(1)}, u32[]{:S(2)}) %copy-start.3) | copy-done | bytes 532504
  41.0 2.7 %pair_sums.1 = (f32[272,256]{1,0:T(8,128)}, bf16[272,256]{1,0:T(8,128)(2,1)}, bf16[272,256]{1,0:T(8,128)(2,1)}, bf16[272,256]{1,0:T(8,128)(2,1)}) custom-call(bf16[272,256]{1,0:T(8,128)(2,1)} %get-tuple-element.17.refs_0_.refs_4_, bf16[272,256]{1,0:T(8,128)(2,1)} %copy-done, bf16[272,256]{1,0:T(8,128)(2,1)} %copy-done.1, bf16[272,256]{1,0:T(8,128)(2,1)} %copy-done.2, ...), custom_call_target="tpu_custom_call" | custom-call | flops 4194304 | bytes 1048576 | tf_op jit(solution)/shard_map/pair_sums/pallas_call | solution.py:318
  43.7 1.9 %collective-permute-start.7 = (bf16[272,256]{1,0:T(8,128)(2,1)}, bf16[272,256]{1,0:T(8,128)(2,1)S(1)}, u32[]{:S(2)}, u32[]{:S(2)}) collective-permute-start(bf16[272,256]{1,0:T(8,128)(2,1)} %get-tuple-element.26), channel_id=1, source_target_pairs={{0,2},{1,3},{2,0},{3,1},{4,6},{5,7},{6,4},{7,5},{8,10},{9,11},{10,... | collective-permute-start | bytes 417800 | tf_op jit(solution)/shard_map/ppermute | solution.py:358
  45.5 3.0 %collective-permute-start.8 = (bf16[272,256]{1,0:T(8,128)(2,1)}, bf16[272,256]{1,0:T(8,128)(2,1)S(1)}, u32[]{:S(2)}, u32[]{:S(2)}) collective-permute-start(bf16[272,256]{1,0:T(8,128)(2,1)} %get-tuple-element.27), channel_id=1, source_target_pairs={{0,4},{1,5},{2,6},{3,7},{4,0},{5,1},{6,2},{7,3},{8,12},{9,13},{10,... | collective-permute-start | bytes 417800 | tf_op jit(solution)/shard_map/ppermute | solution.py:358
  48.6 0.0 collective-permute-start.9
  48.6 1.5 %collective-permute-done.7.refs_1_ = bf16[272,256]{1,0:T(8,128)(2,1)S(1)} collective-permute-done((bf16[272,256]{1,0:T(8,128)(2,1)}, bf16[272,256]{1,0:T(8,128)(2,1)S(1)}, u32[]{:S(2)}, u32[]{:S(2)}) %collective-permute-start.7) | collective-permute-done | bytes 139296 | tf_op jit(solution)/shard_map/ppermute | solution.py:358
  50.1 0.0 copy-start.7
  50.1 5.7 %collective-permute-done.8.refs_2_ = bf16[272,256]{1,0:T(8,128)(2,1)S(1)} collective-permute-done((bf16[272,256]{1,0:T(8,128)(2,1)}, bf16[272,256]{1,0:T(8,128)(2,1)S(1)}, u32[]{:S(2)}, u32[]{:S(2)}) %collective-permute-start.8) | collective-permute-done | bytes 139296 | tf_op jit(solution)/shard_map/ppermute | solution.py:358
  55.8 0.0 copy-start.8
  55.8 0.0 collective-permute-done.9.refs_3_
  55.8 0.0 copy-start.9
  55.9 0.0 copy-done.7
  55.9 0.6 %copy-done.8 = bf16[272,256]{1,0:T(8,128)(2,1)} copy-done((bf16[272,256]{1,0:T(8,128)(2,1)}, bf16[272,256]{1,0:T(8,128)(2,1)S(1)}, u32[]{:S(2)}) %copy-start.8) | copy-done | bytes 139288
  56.5 0.1 copy-done.9
  56.5 2.0 %final.1 = f32[256,256]{1,0:T(8,128)} custom-call(f32[272,256]{1,0:T(8,128)} %get-tuple-element.25.refs_0_, bf16[272,256]{1,0:T(8,128)(2,1)} %copy-done.7, bf16[272,256]{1,0:T(8,128)(2,1)} %copy-done.8, bf16[272,256]{1,0:T(8,128)(2,1)} %copy-done.9), custom_call_target="tpu_custom_call" | custom-call | flops 1048576 | bytes 1048576 | tf_op jit(solution)/shard_map/final/pallas_call | solution.py:318
Async XLA Ops:
  4.8 14.8 %collective-permute-start = (bf16[272,256]{1,0:T(8,128)(2,1)}, bf16[272,256]{1,0:T(8,128)(2,1)S(1)}, u32[]{:S(2)}, u32[]{:S(2)}) collective-permute-start(bf16[272,256]{1,0:T(8,128)(2,1)} %get-tuple-element.18), channel_id=1, source_target_pairs={{0,8},{8,0},{16,24},{24,16},{1,9},{9,1},{17,25},{25,17},{2,10},{10... | collective-permute-start | bytes 417800 | tf_op jit(solution)/shard_map/ppermute | solution.py:307
  7.9 13.7 %collective-permute-start.1 = (bf16[272,256]{1,0:T(8,128)(2,1)}, bf16[272,256]{1,0:T(8,128)(2,1)S(1)}, u32[]{:S(2)}, u32[]{:S(2)}) collective-permute-start(bf16[272,256]{1,0:T(8,128)(2,1)} %get-tuple-element.19), channel_id=1, source_target_pairs={{0,16},{8,24},{16,0},{24,8},{1,17},{9,25},{17,1},{25,9},{2,18},{10... | collective-permute-start | bytes 417800 | tf_op jit(solution)/shard_map/ppermute | solution.py:307
  10.5 11.1 %collective-permute-start.2 = (bf16[272,256]{1,0:T(8,128)(2,1)}, bf16[272,256]{1,0:T(8,128)(2,1)S(1)}, u32[]{:S(2)}, u32[]{:S(2)}) collective-permute-start(bf16[272,256]{1,0:T(8,128)(2,1)} %get-tuple-element.20), channel_id=1, source_target_pairs={{0,24},{8,16},{16,8},{24,0},{1,25},{9,17},{17,9},{25,1},{2,26},{10... | collective-permute-start | bytes 417800 | tf_op jit(solution)/shard_map/ppermute | solution.py:307
  15.2 10.7 %collective-permute-start.3 = (bf16[256,256]{1,0:T(8,128)(2,1)}, bf16[256,256]{1,0:T(8,128)(2,1)S(1)}, u32[]{:S(2)}, u32[]{:S(2)}) collective-permute-start(bf16[256,256]{1,0:T(8,128)(2,1)} %get-tuple-element.22), channel_id=1, source_target_pairs={{0,8},{8,0},{16,24},{24,16},{1,9},{9,1},{17,25},{25,17},{2,10},{10... | collective-permute-start | bytes 393224 | tf_op jit(solution)/shard_map/ppermute | solution.py:307
  16.1 16.9 %collective-permute-start.4 = (bf16[256,256]{1,0:T(8,128)(2,1)}, bf16[256,256]{1,0:T(8,128)(2,1)S(1)}, u32[]{:S(2)}, u32[]{:S(2)}) collective-permute-start(bf16[256,256]{1,0:T(8,128)(2,1)} %get-tuple-element.23), channel_id=1, source_target_pairs={{0,16},{8,24},{16,0},{24,8},{1,17},{9,25},{17,1},{25,9},{2,18},{10... | collective-permute-start | bytes 393224 | tf_op jit(solution)/shard_map/ppermute | solution.py:307
  19.6 2.0 %copy-start = (bf16[272,256]{1,0:T(8,128)(2,1)}, bf16[272,256]{1,0:T(8,128)(2,1)S(1)}, u32[]{:S(2)}) copy-start(bf16[272,256]{1,0:T(8,128)(2,1)S(1)} %collective-permute-done.refs_1_.refs_5_) | copy-start | bytes 417796
  19.6 13.4 %collective-permute-start.5 = (bf16[256,256]{1,0:T(8,128)(2,1)}, bf16[256,256]{1,0:T(8,128)(2,1)S(1)}, u32[]{:S(2)}, u32[]{:S(2)}) collective-permute-start(bf16[256,256]{1,0:T(8,128)(2,1)} %get-tuple-element.24), channel_id=1, source_target_pairs={{0,24},{8,16},{16,8},{24,0},{1,25},{9,17},{17,9},{25,1},{2,26},{10... | collective-permute-start | bytes 393224 | tf_op jit(solution)/shard_map/ppermute | solution.py:307
  21.5 0.7 %copy-start.1 = (bf16[272,256]{1,0:T(8,128)(2,1)}, bf16[272,256]{1,0:T(8,128)(2,1)S(1)}, u32[]{:S(2)}) copy-start(bf16[272,256]{1,0:T(8,128)(2,1)S(1)} %collective-permute-done.1.refs_2_.refs_6_) | copy-start | bytes 417796
  21.5 0.7 %copy-start.2 = (bf16[272,256]{1,0:T(8,128)(2,1)}, bf16[272,256]{1,0:T(8,128)(2,1)S(1)}, u32[]{:S(2)}) copy-start(bf16[272,256]{1,0:T(8,128)(2,1)S(1)} %collective-permute-done.2.refs_3_.refs_7_) | copy-start | bytes 417796
  25.9 7.0 %copy-start.4 = (bf16[256,256]{1,0:T(8,128)(2,1)}, bf16[256,256]{1,0:T(8,128)(2,1)S(1)}, u32[]{:S(2)}) copy-start(bf16[256,256]{1,0:T(8,128)(2,1)S(1)} %collective-permute-done.3.refs_1_) | copy-start | bytes 393220
  32.9 0.7 %copy-start.5 = (bf16[256,256]{1,0:T(8,128)(2,1)}, bf16[256,256]{1,0:T(8,128)(2,1)S(1)}, u32[]{:S(2)}) copy-start(bf16[256,256]{1,0:T(8,128)(2,1)S(1)} %collective-permute-done.4.refs_2_) | copy-start | bytes 393220
  32.9 0.7 %copy-start.6 = (bf16[256,256]{1,0:T(8,128)(2,1)}, bf16[256,256]{1,0:T(8,128)(2,1)S(1)}, u32[]{:S(2)}) copy-start(bf16[256,256]{1,0:T(8,128)(2,1)S(1)} %collective-permute-done.5.refs_3_) | copy-start | bytes 393220
  36.8 3.4 %collective-permute-start.6 = (bf16[1040,256]{1,0:T(8,128)(2,1)}, bf16[1040,256]{1,0:T(8,128)(2,1)S(1)}, u32[]{:S(2)}, u32[]{:S(2)}) collective-permute-start(bf16[1040,256]{1,0:T(8,128)(2,1)} %sums_second_0.1), channel_id=1, source_target_pairs={{0,1},{1,0},{2,3},{3,2},{4,5},{5,4},{6,7},{7,6},{8,9},{9,8},{10,11... | collective-permute-start | bytes 1597448 | tf_op jit(solution)/shard_map/ppermute | solution.py:350
  40.2 0.8 %copy-start.3 = (bf16[1040,256]{1,0:T(8,128)(2,1)}, bf16[1040,256]{1,0:T(8,128)(2,1)S(1)}, u32[]{:S(2)}) copy-start(bf16[1040,256]{1,0:T(8,128)(2,1)S(1)} %collective-permute-done.6.refs_5_) | copy-start | bytes 1597444
  43.7 6.4 %collective-permute-start.7 = (bf16[272,256]{1,0:T(8,128)(2,1)}, bf16[272,256]{1,0:T(8,128)(2,1)S(1)}, u32[]{:S(2)}, u32[]{:S(2)}) collective-permute-start(bf16[272,256]{1,0:T(8,128)(2,1)} %get-tuple-element.26), channel_id=1, source_target_pairs={{0,2},{1,3},{2,0},{3,1},{4,6},{5,7},{6,4},{7,5},{8,10},{9,11},{10,... | collective-permute-start | bytes 417800 | tf_op jit(solution)/shard_map/ppermute | solution.py:358
  45.5 10.3 %collective-permute-start.8 = (bf16[272,256]{1,0:T(8,128)(2,1)}, bf16[272,256]{1,0:T(8,128)(2,1)S(1)}, u32[]{:S(2)}, u32[]{:S(2)}) collective-permute-start(bf16[272,256]{1,0:T(8,128)(2,1)} %get-tuple-element.27), channel_id=1, source_target_pairs={{0,4},{1,5},{2,6},{3,7},{4,0},{5,1},{6,2},{7,3},{8,12},{9,13},{10,... | collective-permute-start | bytes 417800 | tf_op jit(solution)/shard_map/ppermute | solution.py:358
  48.6 7.3 %collective-permute-start.9 = (bf16[272,256]{1,0:T(8,128)(2,1)}, bf16[272,256]{1,0:T(8,128)(2,1)S(1)}, u32[]{:S(2)}, u32[]{:S(2)}) collective-permute-start(bf16[272,256]{1,0:T(8,128)(2,1)} %get-tuple-element.28), channel_id=1, source_target_pairs={{0,6},{1,7},{2,4},{3,5},{4,2},{5,3},{6,0},{7,1},{8,14},{9,15},{10,... | collective-permute-start | bytes 417800 | tf_op jit(solution)/shard_map/ppermute | solution.py:358
  50.1 5.8 %copy-start.7 = (bf16[272,256]{1,0:T(8,128)(2,1)}, bf16[272,256]{1,0:T(8,128)(2,1)S(1)}, u32[]{:S(2)}) copy-start(bf16[272,256]{1,0:T(8,128)(2,1)S(1)} %collective-permute-done.7.refs_1_) | copy-start | bytes 417796
  55.8 0.7 %copy-start.8 = (bf16[272,256]{1,0:T(8,128)(2,1)}, bf16[272,256]{1,0:T(8,128)(2,1)S(1)}, u32[]{:S(2)}) copy-start(bf16[272,256]{1,0:T(8,128)(2,1)S(1)} %collective-permute-done.8.refs_2_) | copy-start | bytes 417796
  55.8 0.7 %copy-start.9 = (bf16[272,256]{1,0:T(8,128)(2,1)}, bf16[272,256]{1,0:T(8,128)(2,1)S(1)}, u32[]{:S(2)}) copy-start(bf16[272,256]{1,0:T(8,128)(2,1)S(1)} %collective-permute-done.9.refs_3_) | copy-start | bytes 417796

commit v2 on v1

v2 whole, which is shorter than its diff:
```python
import functools
import math

import jax
import jax.numpy as jnp
from jax import lax
from jax.experimental import pallas as pl
from jax.experimental.pallas import tpu as pltpu
from jax.sharding import PartitionSpec as P


HEADS = 2
ROWS_DEV = 256
EXTRA = 8
BASE = 128
LIMIT = 24 << 20
NT = (((1,), (1,)), ((), ()))
TN = (((0,), (0,)), ((), ()))


def dot(a, b, dims=(((1,), (0,)), ((), ()))):
    return lax.dot_general(a, b, dims, preferred_element_type=jnp.float32)


def digits_row(total, width):
    lane = lax.broadcasted_iota(jnp.int32, (1, width), 1)
    low, mid, high = total % BASE, (total // BASE) % BASE, total // (BASE * BASE)
    row = jnp.where(lane == 0, low, jnp.where(lane == 1, mid, jnp.where(lane == 2, high, 0)))
    return row.astype(jnp.float32)


def total_of_digits(row):
    return row[:, 0:1] + row[:, 1:2] * float(BASE) + row[:, 2:3] * float(BASE * BASE)


def attention_kernel(
    half, halves, groups, tile, extra,
    len_h, own_h, emb_h, gout_h, wq_h, wk_h, wv_h, rows_h, *refs,
):
    outs = refs[:groups]
    (emb, gout, wq, wk, wv, rows, len_ref, own_ref,
     q_s, k_s, v_s, dq_s, dk_s, dv_s, tok_s, ext_s, idx_s, sems) = refs[groups:]
    width = emb.shape[1]
    half_seqs = len_ref.shape[0] // halves
    half_tiles = own_ref.shape[0] // halves
    span = emb.shape[0] // half_seqs
    head = width // HEADS
    scale = 1.0 / math.sqrt(head)
    block = span // 2
    start = half * half_seqs * span

    def piece(s):
        return pl.ds(s * span, span)

    plan = [(len_h, len_ref)]
    plan += [(emb_h.at[pl.ds(start, span)], emb.at[piece(0)]), (wq_h, wq), (wk_h, wk), (wv_h, wv)]
    plan += [(gout_h.at[pl.ds(start, span)], gout.at[piece(0)])]
    for s in range(1, half_seqs):
        plan += [
            (emb_h.at[pl.ds(start + s * span, span)], emb.at[piece(s)]),
            (gout_h.at[pl.ds(start + s * span, span)], gout.at[piece(s)]),
        ]
    plan += [(own_h, own_ref), (rows_h, rows)]
    copies = [pltpu.make_async_copy(a, b, sems.at[i]) for i, (a, b) in enumerate(plan)]
    for c in copies:
        c.start()

    def gate(raw, grad, weight):
        grown = jnp.exp(raw * (-scale))
        sigma = 1.0 / (1.0 + grown)
        act = raw * scale * sigma
        slope = sigma + act * (1.0 - sigma)
        return (
            (act * weight).astype(jnp.bfloat16),
            (grad * weight * slope).astype(jnp.bfloat16),
        )

    def run(base, count, live):
        def rows_of(ref, at, size):
            return ref[base + at:base + at + size, :]

        q_s[0:live, :] = dot(rows_of(emb, 0, live), wq[...]).astype(jnp.bfloat16)
        k_s[0:live, :] = dot(rows_of(emb, 0, live), wk[...]).astype(jnp.bfloat16)
        v_s[0:live, :] = dot(rows_of(emb, 0, live), wv[...]).astype(jnp.bfloat16)
        lane = lax.broadcasted_iota(jnp.int32, (1, block), 1)
        inverse = 1.0 / jnp.broadcast_to(count, (1, block)).astype(jnp.float32)
        sub = lax.broadcasted_iota(jnp.int32, (block, block), 0)
        lan = lax.broadcasted_iota(jnp.int32, (block, block), 1)
        causal = sub <= lan
        for h in range(HEADS):
            cols = slice(h * head, (h + 1) * head)
            att, sco = {}, {}
            for i in range(live // block):
                weight = jnp.where(lane + i * block < count, inverse, 0.0)
                iq = q_s[i * block:(i + 1) * block, cols]
                ig = gout[base + i * block:base + (i + 1) * block, cols]
                for j in range(i + 1):
                    jk = k_s[j * block:(j + 1) * block, cols]
                    jv = v_s[j * block:(j + 1) * block, cols]
                    raw = dot(jk, iq, NT)
                    grad = dot(jv, ig, NT)
                    if i == j:
                        use = jnp.where(causal, weight, 0.0)
                    else:
                        use = weight
                    att[j, i], sco[j, i] = gate(raw, grad, use)
            for j in range(live // block):
                vg = kg = None
                for i in range(j, live // block):
                    iq = q_s[i * block:(i + 1) * block, cols]
                    ig = gout[base + i * block:base + (i + 1) * block, cols]
                    a, b = dot(att[j, i], ig), dot(sco[j, i], iq)
                    vg = a if vg is None else vg + a
                    kg = b if kg is None else kg + b
                dv_s[j * block:(j + 1) * block, cols] = vg.astype(jnp.bfloat16)
                dk_s[j * block:(j + 1) * block, cols] = (kg * scale).astype(jnp.bfloat16)
            for i in range(live // block):
                qg = None
                for j in range(i + 1):
                    jk = k_s[j * block:(j + 1) * block, cols]
                    c = dot(sco[j, i], jk, TN)
                    qg = c if qg is None else qg + c
                dq_s[i * block:(i + 1) * block, cols] = (qg * scale).astype(jnp.bfloat16)
        token = dot(dq_s[0:live, :], wq[...], NT)
        token = token + dot(dk_s[0:live, :], wk[...], NT)
        token = token + dot(dv_s[0:live, :], wv[...], NT)
        tok_s[base:base + live, :] = token.astype(jnp.bfloat16)
        if live < span:
            tok_s[base + live:base + span, :] = jnp.zeros((span - live, width), jnp.bfloat16)

    for c in copies[:6]:
        c.wait()
    for s in range(half_seqs):
        if s:
            for c in copies[4 + 2 * s:6 + 2 * s]:
                c.wait()
        count = len_ref[half * half_seqs + s]
        pl.when(count <= block)(functools.partial(run, s * span, count, block))
        pl.when(count > block)(functools.partial(run, s * span, count, span))
    for c in copies[-2:]:
        c.wait()

    me = lax.axis_index("group")
    owned = half_tiles // groups

    def place(part):
        for g in range(groups):
            idx_s[groups * owned + g] = 0
        for t in range(half_tiles):
            owner = own_ref[part * half_tiles + t]
            seen = idx_s[groups * owned + owner]
            idx_s[owner * owned + seen] = t
            idx_s[groups * owned + owner] = seen + 1

    if extra:
        total = len_ref[0]
        for s in range(1, len_ref.shape[0]):
            total = total + len_ref[s]
        for k in range(groups):
            ext_s[k] = jnp.zeros(ext_s.shape[1:], jnp.float32)
            ext_s[k, halves * owned:halves * owned + 1, :] = digits_row(total, width)
        for part in range(halves):
            place(part)
            for k in range(groups):
                owner = me ^ k
                for s in range(owned):
                    t = idx_s[owner * owned + s] + part * half_tiles
                    row = rows[pl.ds(t, 1), :]
                    at = part * owned + s
                    ext_s[k, at:at + 1, 0:tile] = (row // ROWS_DEV).astype(jnp.float32)
                    ext_s[k, at:at + 1, tile:2 * tile] = (row % ROWS_DEV).astype(jnp.float32)
        for k in range(groups):
            outs[k][owned * tile:owned * tile + EXTRA, :] = ext_s[k].astype(jnp.bfloat16)
    place(half)
    for k in range(groups):
        owner = me ^ k
        for s in range(owned):
            t = idx_s[owner * owned + s]
            outs[k][s * tile:(s + 1) * tile, :] = tok_s[
                pl.ds(pl.multiple_of(t * tile, tile), tile), :
            ]


def attention(half, halves, groups, lengths, owners, embeds, out_grad, wq, wk, wv, rows, extra):
    tokens, width = embeds.shape
    seqs = lengths.shape[0]
    span = tokens // seqs
    tile = tokens // owners.shape[0]
    half_seqs, half_tiles = seqs // halves, owners.shape[0] // halves
    owned = half_tiles // groups
    out_rows = owned * tile + (EXTRA if extra else 0)
    flops = half_seqs * (2 * span * width * width * 6 + 10 * span * span * width)
    bf16 = jnp.bfloat16
    return pl.pallas_call(
        functools.partial(attention_kernel, half, halves, groups, tile, extra),
        in_specs=[pl.BlockSpec(memory_space=pltpu.HBM)] * 8,
        out_specs=vmem(groups),
        out_shape=[jax.ShapeDtypeStruct((out_rows, width), bf16)] * groups,
        scratch_shapes=[pltpu.VMEM((half_seqs * span, width), bf16)] * 2
        + [pltpu.VMEM((width, width), bf16)] * 3
        + [
            pltpu.VMEM(rows.shape, jnp.int32),
            pltpu.SMEM(lengths.shape, jnp.int32),
            pltpu.SMEM(owners.shape, jnp.int32),
        ]
        + [pltpu.VMEM((span, width), bf16)] * 6
        + [
            pltpu.VMEM((half_seqs * span, width), bf16),
            pltpu.VMEM((groups, EXTRA, width), jnp.float32),
            pltpu.SMEM((groups * owned + groups,), jnp.int32),
            pltpu.SemaphoreType.DMA((6 + 2 * half_seqs,)),
        ],
        compiler_params=pltpu.CompilerParams(vmem_limit_bytes=LIMIT),
        cost_estimate=pl.CostEstimate(
            flops=flops, bytes_accessed=4 * half_seqs * span * width * 2, transcendentals=0
        ),
    )(*[
        pltpu.with_memory_space_constraint(a, pltpu.HBM)
        for a in (lengths, owners, embeds, out_grad, wq, wk, wv, rows)
    ])


def sums_of(block, boxes, exts, first, owned, tile):
    total = None
    row = lax.broadcasted_iota(jnp.int32, (ROWS_DEV, owned * tile), 0).astype(jnp.float32)
    for box, ext in zip(boxes, exts):
        slots = [ext[first + s:first + s + 1, :].astype(jnp.float32) for s in range(owned)]
        high = jnp.concatenate([r[:, 0:tile] for r in slots], axis=1)
        low = jnp.concatenate([r[:, tile:2 * tile] for r in slots], axis=1)
        key = jnp.where(high == block.astype(jnp.float32), low, -1.0)
        hot = jnp.where(row == key, 1.0, 0.0).astype(jnp.bfloat16)
        part = dot(hot, box[0:owned * tile, :])
        total = part if total is None else total + part
    return total


def live_of(exts, at):
    total = None
    for e in exts:
        row = total_of_digits(e[at:at + 1, :].astype(jnp.float32))
        total = row if total is None else total + row
    return total


def live_rows(total, like):
    width = like.shape[-1]
    row = digits_row(jnp.broadcast_to(total, (1, width)).astype(jnp.int32), width)
    return jnp.broadcast_to(row, (EXTRA, width)).astype(like.dtype)


def exts_of(boxes, base):
    return [b[base:base + EXTRA, :] for b in boxes]


def first_kernel(pairs, owned, tile, *refs):
    boxes, acc = refs[:-1], refs[-1]
    core = lax.axis_index("batch") % 2
    exts = exts_of(boxes, owned * tile)
    for side in range(2):
        for p in range(pairs):
            block = 2 * p + (1 - core if side == 0 else core)
            acc[side, p] = sums_of(block, boxes, exts, 0, owned, tile)


def side_kernel(side, pairs, owned, tile, heads, bodies, *refs):
    acc = refs[heads + bodies] if len(refs) > heads + bodies + 1 else None
    head, body, out = refs[:heads], refs[heads:heads + bodies], refs[-1]
    core = lax.axis_index("batch") % 2
    exts = exts_of(head, owned * tile)
    for p in range(pairs):
        block = 2 * p + (1 - core if side == 0 else core)
        total = sums_of(block, body, exts, owned, owned, tile)
        if acc is None:
            total = total + sums_of(block, head, exts, 0, owned, tile)
        else:
            total = total + acc[0, p]
        out[p * ROWS_DEV:(p + 1) * ROWS_DEV, :] = total.astype(out.dtype)
    if side == 0:
        out[pairs * ROWS_DEV:pairs * ROWS_DEV + EXTRA, :] = live_rows(
            live_of(exts, 2 * owned), out
        )


def pair_kernel(pairs, owned, tile, heads, *refs):
    head, own, got = refs[:heads], refs[heads], refs[heads + 1]
    outs = refs[heads + 2:]
    pair = lax.axis_index("batch") // 2
    live = live_of(exts_of(head, owned * tile), 2 * owned)
    live = live + live_of([got[pairs * ROWS_DEV:pairs * ROWS_DEV + 1, :]], 0)
    for k in range(pairs):
        at = pl.multiple_of((pair ^ k) * ROWS_DEV, ROWS_DEV)
        total = own[pl.ds(at, ROWS_DEV), :] + got[pl.ds(at, ROWS_DEV), :].astype(jnp.float32)
        outs[k][0:ROWS_DEV, :] = total.astype(outs[k].dtype)
        outs[k][ROWS_DEV:ROWS_DEV + EXTRA, :] = live_rows(live, outs[k])


def gathered(ins):
    total = live = None
    for r in ins:
        part = r[0:ROWS_DEV, :].astype(jnp.float32)
        some = total_of_digits(r[ROWS_DEV:ROWS_DEV + 1, :].astype(jnp.float32))
        total = part if total is None else total + part
        live = some if live is None else live + some
    return total, live


def far_kernel(*refs):
    total, live = gathered(refs[:-1])
    out = refs[-1]
    out[0:ROWS_DEV, :] = total.astype(out.dtype)
    out[ROWS_DEV:ROWS_DEV + EXTRA, :] = live_rows(live, out)


def last_kernel(tokens_all, *refs):
    total, live = gathered(refs[:-1])
    refs[-1][...] = total * (tokens_all / live)


def vmem(n):
    return [pl.BlockSpec(memory_space=pltpu.VMEM)] * n


def call(kernel, shapes, flops, *args):
    return pl.pallas_call(
        kernel,
        in_specs=vmem(len(args)),
        out_specs=vmem(len(shapes)) if isinstance(shapes, list) else vmem(1)[0],
        out_shape=shapes,
        compiler_params=pltpu.CompilerParams(vmem_limit_bytes=LIMIT),
        cost_estimate=pl.CostEstimate(flops=flops, bytes_accessed=1 << 20, transcendentals=0),
    )(*args)


def on_device(groups, batches, embeds, out_grad, w_query, w_key, w_value, lengths, item_rows,
              tile_owner):
    tokens, width = embeds.shape
    halves = 2
    tile = tokens // tile_owner.shape[0]
    owned = tile_owner.shape[0] // halves // groups
    pairs = batches // 2
    rows = item_rows.reshape(-1, tile)
    f32, bf16 = jnp.float32, jnp.bfloat16
    shape = jax.ShapeDtypeStruct
    far = groups - 1
    work = 2 * pairs * ROWS_DEV * width * owned * tile

    def swap(box, k):
        return lax.ppermute(box, "group", [(i, i ^ k) for i in range(groups)])

    def across(box, k):
        return lax.ppermute(box, "batch", [(i, i ^ k) for i in range(batches)])

    near, away = [], []
    for half in range(halves):
        mine = list(attention(
            half, halves, groups, lengths, tile_owner, embeds, out_grad,
            w_query, w_key, w_value, rows, half == 0,
        ))
        near.append([mine[0]] + [swap(mine[k], k) for k in range(far - 1, 0, -1)])
        away.append([mine[far]])

    def side(which, flops, heads, bodies, acc=None):
        out = shape((pairs * ROWS_DEV + EXTRA, width), bf16) if which == 0 else shape(
            (pairs * ROWS_DEV, width), f32)
        specs = vmem(len(heads) + len(bodies))
        args = [*heads, *bodies]
        if acc is not None:
            specs = specs + [
                pl.BlockSpec((1, pairs, ROWS_DEV, width), lambda s: (which, 0, 0, 0))
            ]
            args = args + [acc]
        return pl.pallas_call(
            functools.partial(
                side_kernel, which, pairs, owned, tile, len(heads), len(bodies)
            ),
            grid=(1,),
            in_specs=specs,
            out_specs=vmem(1)[0],
            out_shape=out,
            compiler_params=pltpu.CompilerParams(vmem_limit_bytes=LIMIT),
            cost_estimate=pl.CostEstimate(
                flops=flops, bytes_accessed=1 << 20, transcendentals=0
            ),
        )(*args)

    def plane(heads, bodies, acc=None):
        flops = work * (len(bodies) + (len(heads) if acc is None else 0))
        send = side(0, flops, heads, bodies, acc)
        got = across(send, 1)
        own = side(1, flops, heads, bodies, acc)
        parts = call(
            functools.partial(pair_kernel, pairs, owned, tile, len(heads)),
            [shape((ROWS_DEV + EXTRA, width), f32 if k == 0 else bf16) for k in range(pairs)],
            1 << 22, *heads, own, got,
        )
        return [parts[0]] + [across(parts[k], 2 * k) for k in range(1, pairs)]

    far_parts = plane(away[0], away[1])
    acc = call(
        functools.partial(first_kernel, pairs, owned, tile),
        shape((2, pairs, ROWS_DEV, width), f32), 2 * far * work, *near[0],
    )
    near_parts = plane(near[0], near[1], acc)
    far_sum = call(far_kernel, shape((ROWS_DEV + EXTRA, width), bf16), 1 << 20, *far_parts)
    return call(
        functools.partial(last_kernel, float(tokens * groups * batches)),
        shape((ROWS_DEV, width), f32), 1 << 20, *near_parts, swap(far_sum, far),
    )


def solution(mesh):
    groups, batches = mesh.shape["group"], mesh.shape["batch"]
    both = P(("group", "batch"))
    wide = P(("group", "batch"), None)

    def body(*args):
        return on_device(groups, batches, *args)

    return jax.shard_map(
        body,
        mesh=mesh,
        in_specs=(wide, wide, P(), P(), P(), both, both, both),
        out_specs=wide,
        check_vma=False,
    )
```

time: 58.8 us -> 49 us (0.83)
  Pallas kernels: 24.4 us -> 12.7 us
  starting transfers between devices: 15 us -> 18.2 us
  local copies, waits for them, and re-layouts: 2.88 us -> 0 us
  waiting for transfers between devices: 16.2 us -> 17.8 us
    pallas_call x4 -> x6, Pallas kernels: 16 us -> 10.2 us  [the longest x2 8.17 us: attention(): pl.pallas_call(functools.partial(attention_kernel, half, halves, groups,...]
    pallas_call x3 -> x5, Pallas kernels: 8.38 us -> 2.54 us  [call(): pl.pallas_call(kernel, in_specs=vmem(len(args)), out_specs=vmem(len(shape...]
    ppermute x4 -> x8, starting transfers between devices: 4.92 us -> 10.7 us  [across(): return lax.ppermute(box, 'batch', [(i, i ^ k) for i in range(batches)])]
    unnamed x20 -> x0, local copies, waits for them, and re-layouts: 2.88 us -> none
    ppermute x6 -> x5, starting transfers between devices: 10.1 us -> 7.53 us  [swap(): return lax.ppermute(box, 'group', [(i, i ^ k) for i in range(groups)])]
    ppermute x4 -> x8, waiting for transfers between devices: 7.25 us -> 9.73 us  [across(): return lax.ppermute(box, 'batch', [(i, i ^ k) for i in range(batches)])]
    ppermute x6 -> x5, waiting for transfers between devices: 8.98 us -> 8.09 us  [swap(): return lax.ppermute(box, 'group', [(i, i ^ k) for i in range(groups)])]
  transfers between devices with their start and end apart: 10 -> 13, of which waited for: 4 -> 6; matrix products, arithmetic and copies ran while one was open for 0% -> 0% of each run, Pallas kernels for 20% -> 16%
where the time goes in v2:
time: 49 us; the launch traced here: 48.9 us
  starting transfers between devices  18.2 us (37%)
  waiting for transfers between devices  17.8 us (36%)
  Pallas kernels  12.7 us (26%)
    ppermute x8, starting transfers between devices, across(): return lax.ppermute(box, 'batch', [(i, i ^ k) for i in range(batches)])  10.7 us
    ppermute x8, waiting for transfers between devices, across(): return lax.ppermute(box, 'batch', [(i, i ^ k) for i in range(batches)])  9.73 us
    pallas_call x2, Pallas kernels, attention(): pl.pallas_call(functools.partial(attention_kernel, half, halves, groups,...  8.17 us
    ppermute x5, waiting for transfers between devices, swap(): return lax.ppermute(box, 'group', [(i, i ^ k) for i in range(groups)])  8.09 us
    ppermute x5, starting transfers between devices, swap(): return lax.ppermute(box, 'group', [(i, i ^ k) for i in range(groups)])  7.53 us
    pallas_call x5, Pallas kernels, call(): pl.pallas_call(kernel, in_specs=vmem(len(args)), out_specs=vmem(len(shape...  2.54 us
    pallas_call x4, Pallas kernels, side(): pl.pallas_call(functools.partial(side_kernel, which, pairs, owned, tile,...  2.01 us
  transfers between devices with their start and end apart: 13, of which 6 were waited for; matrix products, arithmetic and copies ran while one was open for 0% of the time, Pallas kernels for 16%

profile of v2, /device:TPU:0, one launch (start us, length us, event | category | flops | bytes accessed | tf_op | source)
XLA Modules:
  0.0 48.9 jit_solution(1868877160339447994)
XLA Ops:
  0.0 4.1 %shard_map.82 = (bf16[264,256]{1,0:T(8,128)(2,1)S(1)}, bf16[264,256]{1,0:T(8,128)(2,1)S(1)}, bf16[264,256]{1,0:T(8,128)(2,1)S(1)}, bf16[264,256]{1,0:T(8,128)(2,1)S(1)}) custom-call(s32[4]{0:T(128)} %len_h.3, s32[16]{0:T(128)} %own_h.3, bf16[2048,256]{1,0:T(8,128)(2,1)} %emb_h.3, bf16[2048,256]{1,0:T(8,128)(2,1)} %gout_h.3, bf16[256,256]{1,0:T(8,128)(2,1)} %wq_h.3, ...), custom_call_target="tpu_custom_call" | custom-call | flops 2147483648 | bytes 2097152 | tf_op jit(solution)/shard_map/pallas_call | solution.py:194
  4.1 4.1 %collective-permute-start = (bf16[264,256]{1,0:T(8,128)(2,1)S(1)}, bf16[264,256]{1,0:T(8,128)(2,1)S(1)}, u32[]{:S(2)}, u32[]{:S(2)}) collective-permute-start(bf16[264,256]{1,0:T(8,128)(2,1)S(1)} %get-tuple-element.22), channel_id=1, source_target_pairs={{0,16},{8,24},{16,0},{24,8},{1,17},{9,25},{17,1},{25,9},{2,18},{10... | collective-permute-start | bytes 405512 | tf_op jit(solution)/shard_map/ppermute | solution.py:348
  8.2 1.6 %collective-permute-start.1 = (bf16[264,256]{1,0:T(8,128)(2,1)S(1)}, bf16[264,256]{1,0:T(8,128)(2,1)S(1)}, u32[]{:S(2)}, u32[]{:S(2)}) collective-permute-start(bf16[264,256]{1,0:T(8,128)(2,1)S(1)} %get-tuple-element.23), channel_id=1, source_target_pairs={{0,8},{8,0},{16,24},{24,16},{1,9},{9,1},{17,25},{25,17},{2,10},{10... | collective-permute-start | bytes 405512 | tf_op jit(solution)/shard_map/ppermute | solution.py:348
  9.8 4.1 %shard_map.83 = (bf16[256,256]{1,0:T(8,128)(2,1)S(1)}, bf16[256,256]{1,0:T(8,128)(2,1)S(1)}, bf16[256,256]{1,0:T(8,128)(2,1)S(1)}, bf16[256,256]{1,0:T(8,128)(2,1)S(1)}) custom-call(s32[4]{0:T(128)} %len_h.3, s32[16]{0:T(128)} %own_h.3, bf16[2048,256]{1,0:T(8,128)(2,1)} %emb_h.3, bf16[2048,256]{1,0:T(8,128)(2,1)} %gout_h.3, bf16[256,256]{1,0:T(8,128)(2,1)} %wq_h.3, ...), custom_call_target="tpu_custom_call" | custom-call | flops 2147483648 | bytes 2097152 | tf_op jit(solution)/shard_map/pallas_call | solution.py:194
  13.9 0.4 collective-permute-start.2
  14.3 0.2 collective-permute-start.3
  14.5 0.4 shard_map.89
  14.9 0.1 collective-permute-start.8
  15.0 0.0 collective-permute-done.refs_1_
  15.0 0.0 collective-permute-done.1.refs_2_
  15.0 1.0 %shard_map.84.refs_6_ = f32[2,4,256,256]{3,2,1,0:T(8,128)S(1)} custom-call(bf16[264,256]{1,0:T(8,128)(2,1)S(1)} %get-tuple-element.21.refs_0_, bf16[264,256]{1,0:T(8,128)(2,1)S(1)} %collective-permute-done.refs_1_, bf16[264,256]{1,0:T(8,128)(2,1)S(1)} %collective-permute-done.1.refs_2_), custom_call_target="tpu_custom_call" | custom-call | flops 805306368 | bytes 1048576 | tf_op jit(solution)/shard_map/pallas_call | solution.py:324
  16.0 6.2 %collective-permute-done.2.refs_4_ = bf16[256,256]{1,0:T(8,128)(2,1)S(1)} collective-permute-done((bf16[256,256]{1,0:T(8,128)(2,1)S(1)}, bf16[256,256]{1,0:T(8,128)(2,1)S(1)}, u32[]{:S(2)}, u32[]{:S(2)}) %collective-permute-start.2) | collective-permute-done | bytes 131104 | tf_op jit(solution)/shard_map/ppermute | solution.py:348
  22.2 0.0 collective-permute-done.3.refs_5_
  22.2 0.6 %shard_map.86 = bf16[1032,256]{1,0:T(8,128)(2,1)S(1)} custom-call(bf16[264,256]{1,0:T(8,128)(2,1)S(1)} %get-tuple-element.21.refs_0_, bf16[264,256]{1,0:T(8,128)(2,1)S(1)} %collective-permute-done.refs_1_, bf16[264,256]{1,0:T(8,128)(2,1)S(1)} %collective-permute-done.1.refs_2_, bf16[256,256]{1,0:T(8,128)(2,1)S(1)} %get-tuple-element.24.refs_3_, ...), custom_call_target="tpu_custom_call" | custom-call | flops 402653184 | bytes 1048576 | tf_op jit(solution)/shard_map/pallas_call | solution.py:372
  22.8 0.1 collective-permute-start.4
  22.9 0.4 shard_map.88.refs_1_
  23.3 0.0 collective-permute-done.8.refs_2_
  23.3 0.2 shard_map.90
  23.6 3.5 %collective-permute-start.9 = (bf16[264,256]{1,0:T(8,128)(2,1)S(1)}, bf16[264,256]{1,0:T(8,128)(2,1)S(1)}, u32[]{:S(2)}, u32[]{:S(2)}) collective-permute-start(bf16[264,256]{1,0:T(8,128)(2,1)S(1)} %get-tuple-element.34), channel_id=1, source_target_pairs={{0,2},{1,3},{2,0},{3,1},{4,6},{5,7},{6,4},{7,5},{8,10},{9,11},{10,... | collective-permute-start | bytes 405512 | tf_op jit(solution)/shard_map/ppermute | solution.py:351
  27.1 3.5 %collective-permute-start.10 = (bf16[264,256]{1,0:T(8,128)(2,1)S(1)}, bf16[264,256]{1,0:T(8,128)(2,1)S(1)}, u32[]{:S(2)}, u32[]{:S(2)}) collective-permute-start(bf16[264,256]{1,0:T(8,128)(2,1)S(1)} %get-tuple-element.35), channel_id=1, source_target_pairs={{0,4},{1,5},{2,6},{3,7},{4,0},{5,1},{6,2},{7,3},{8,12},{9,13},{10,... | collective-permute-start | bytes 405512 | tf_op jit(solution)/shard_map/ppermute | solution.py:351
  30.6 0.0 collective-permute-start.11
  30.6 0.6 %shard_map.85.refs_3_ = f32[1024,256]{1,0:T(8,128)S(1)} custom-call(bf16[264,256]{1,0:T(8,128)(2,1)S(1)} %get-tuple-element.21.refs_0_, bf16[264,256]{1,0:T(8,128)(2,1)S(1)} %collective-permute-done.refs_1_, bf16[264,256]{1,0:T(8,128)(2,1)S(1)} %collective-permute-done.1.refs_2_, bf16[256,256]{1,0:T(8,128)(2,1)S(1)} %get-tuple-element.24.refs_3_, ...), custom_call_target="tpu_custom_call" | custom-call | flops 402653184 | bytes 1048576 | tf_op jit(solution)/shard_map/pallas_call | solution.py:372
  31.2 0.1 collective-permute-done.9.refs_1_
  31.3 6.2 %collective-permute-done.10.refs_2_ = bf16[264,256]{1,0:T(8,128)(2,1)S(1)} collective-permute-done((bf16[264,256]{1,0:T(8,128)(2,1)S(1)}, bf16[264,256]{1,0:T(8,128)(2,1)S(1)}, u32[]{:S(2)}, u32[]{:S(2)}) %collective-permute-start.10) | collective-permute-done | bytes 135200 | tf_op jit(solution)/shard_map/ppermute | solution.py:351
  37.4 0.0 collective-permute-done.11.refs_3_
  37.4 0.2 shard_map.91
  37.7 1.2 %collective-permute-start.12 = (bf16[264,256]{1,0:T(8,128)(2,1)S(1)}, bf16[264,256]{1,0:T(8,128)(2,1)S(1)}, u32[]{:S(2)}, u32[]{:S(2)}) collective-permute-start(bf16[264,256]{1,0:T(8,128)(2,1)S(1)} %shard_map.91), channel_id=1, source_target_pairs={{0,24},{8,16},{16,8},{24,0},{1,25},{9,17},{17,9},{25,1},{2,26},{10... | collective-permute-start | bytes 405512 | tf_op jit(solution)/shard_map/ppermute | solution.py:348
  38.9 0.0 collective-permute-done.4.refs_4_
  38.9 0.2 shard_map.87
  39.1 1.2 %collective-permute-start.5 = (bf16[264,256]{1,0:T(8,128)(2,1)S(1)}, bf16[264,256]{1,0:T(8,128)(2,1)S(1)}, u32[]{:S(2)}, u32[]{:S(2)}) collective-permute-start(bf16[264,256]{1,0:T(8,128)(2,1)S(1)} %get-tuple-element.28), channel_id=1, source_target_pairs={{0,2},{1,3},{2,0},{3,1},{4,6},{5,7},{6,4},{7,5},{8,10},{9,11},{10,... | collective-permute-start | bytes 405512 | tf_op jit(solution)/shard_map/ppermute | solution.py:351
  40.3 1.2 %collective-permute-start.6 = (bf16[264,256]{1,0:T(8,128)(2,1)S(1)}, bf16[264,256]{1,0:T(8,128)(2,1)S(1)}, u32[]{:S(2)}, u32[]{:S(2)}) collective-permute-start(bf16[264,256]{1,0:T(8,128)(2,1)S(1)} %get-tuple-element.29), channel_id=1, source_target_pairs={{0,4},{1,5},{2,6},{3,7},{4,0},{5,1},{6,2},{7,3},{8,12},{9,13},{10,... | collective-permute-start | bytes 405512 | tf_op jit(solution)/shard_map/ppermute | solution.py:351
  41.5 1.2 %collective-permute-start.7 = (bf16[264,256]{1,0:T(8,128)(2,1)S(1)}, bf16[264,256]{1,0:T(8,128)(2,1)S(1)}, u32[]{:S(2)}, u32[]{:S(2)}) collective-permute-start(bf16[264,256]{1,0:T(8,128)(2,1)S(1)} %get-tuple-element.30), channel_id=1, source_target_pairs={{0,6},{1,7},{2,4},{3,5},{4,2},{5,3},{6,0},{7,1},{8,14},{9,15},{10,... | collective-permute-start | bytes 405512 | tf_op jit(solution)/shard_map/ppermute | solution.py:351
  42.7 1.9 %collective-permute-done.12.refs_4_ = bf16[264,256]{1,0:T(8,128)(2,1)S(1)} collective-permute-done((bf16[264,256]{1,0:T(8,128)(2,1)S(1)}, bf16[264,256]{1,0:T(8,128)(2,1)S(1)}, u32[]{:S(2)}, u32[]{:S(2)}) %collective-permute-start.12) | collective-permute-done | bytes 135200 | tf_op jit(solution)/shard_map/ppermute | solution.py:348
  44.6 0.7 %collective-permute-done.5.refs_1_ = bf16[264,256]{1,0:T(8,128)(2,1)S(1)} collective-permute-done((bf16[264,256]{1,0:T(8,128)(2,1)S(1)}, bf16[264,256]{1,0:T(8,128)(2,1)S(1)}, u32[]{:S(2)}, u32[]{:S(2)}) %collective-permute-start.5) | collective-permute-done | bytes 135200 | tf_op jit(solution)/shard_map/ppermute | solution.py:351
  45.3 2.7 %collective-permute-done.6.refs_2_ = bf16[264,256]{1,0:T(8,128)(2,1)S(1)} collective-permute-done((bf16[264,256]{1,0:T(8,128)(2,1)S(1)}, bf16[264,256]{1,0:T(8,128)(2,1)S(1)}, u32[]{:S(2)}, u32[]{:S(2)}) %collective-permute-start.6) | collective-permute-done | bytes 135200 | tf_op jit(solution)/shard_map/ppermute | solution.py:351
  48.0 0.0 collective-permute-done.7.refs_3_
  48.0 0.9 %shard_map.92 = f32[256,256]{1,0:T(8,128)} custom-call(f32[264,256]{1,0:T(8,128)S(1)} %get-tuple-element.27.refs_0_, bf16[264,256]{1,0:T(8,128)(2,1)S(1)} %collective-permute-done.5.refs_1_, bf16[264,256]{1,0:T(8,128)(2,1)S(1)} %collective-permute-done.6.refs_2_, bf16[264,256]{1,0:T(8,128)(2,1)S(1)} %collective-permute-done.7.refs_3_, ...), custom_call_target="tpu_custom_call" | custom-call | flops 1048576 | bytes 1048576 | tf_op jit(solution)/shard_map/pallas_call | solution.py:324
Async XLA Ops:
  4.1 11.0 %collective-permute-start = (bf16[264,256]{1,0:T(8,128)(2,1)S(1)}, bf16[264,256]{1,0:T(8,128)(2,1)S(1)}, u32[]{:S(2)}, u32[]{:S(2)}) collective-permute-start(bf16[264,256]{1,0:T(8,128)(2,1)S(1)} %get-tuple-element.22), channel_id=1, source_target_pairs={{0,16},{8,24},{16,0},{24,8},{1,17},{9,25},{17,1},{25,9},{2,18},{10... | collective-permute-start | bytes 405512 | tf_op jit(solution)/shard_map/ppermute | solution.py:348
  8.2 6.8 %collective-permute-start.1 = (bf16[264,256]{1,0:T(8,128)(2,1)S(1)}, bf16[264,256]{1,0:T(8,128)(2,1)S(1)}, u32[]{:S(2)}, u32[]{:S(2)}) collective-permute-start(bf16[264,256]{1,0:T(8,128)(2,1)S(1)} %get-tuple-element.23), channel_id=1, source_target_pairs={{0,8},{8,0},{16,24},{24,16},{1,9},{9,1},{17,25},{25,17},{2,10},{10... | collective-permute-start | bytes 405512 | tf_op jit(solution)/shard_map/ppermute | solution.py:348
  13.9 8.3 %collective-permute-start.2 = (bf16[256,256]{1,0:T(8,128)(2,1)S(1)}, bf16[256,256]{1,0:T(8,128)(2,1)S(1)}, u32[]{:S(2)}, u32[]{:S(2)}) collective-permute-start(bf16[256,256]{1,0:T(8,128)(2,1)S(1)} %get-tuple-element.25), channel_id=1, source_target_pairs={{0,16},{8,24},{16,0},{24,8},{1,17},{9,25},{17,1},{25,9},{2,18},{10... | collective-permute-start | bytes 393224 | tf_op jit(solution)/shard_map/ppermute | solution.py:348
  14.3 7.9 %collective-permute-start.3 = (bf16[256,256]{1,0:T(8,128)(2,1)S(1)}, bf16[256,256]{1,0:T(8,128)(2,1)S(1)}, u32[]{:S(2)}, u32[]{:S(2)}) collective-permute-start(bf16[256,256]{1,0:T(8,128)(2,1)S(1)} %get-tuple-element.26), channel_id=1, source_target_pairs={{0,8},{8,0},{16,24},{24,16},{1,9},{9,1},{17,25},{25,17},{2,10},{10... | collective-permute-start | bytes 393224 | tf_op jit(solution)/shard_map/ppermute | solution.py:348
  14.9 8.4 %collective-permute-start.8 = (bf16[1032,256]{1,0:T(8,128)(2,1)S(1)}, bf16[1032,256]{1,0:T(8,128)(2,1)S(1)}, u32[]{:S(2)}, u32[]{:S(2)}) collective-permute-start(bf16[1032,256]{1,0:T(8,128)(2,1)S(1)} %shard_map.89), channel_id=1, source_target_pairs={{0,1},{1,0},{2,3},{3,2},{4,5},{5,4},{6,7},{7,6},{8,9},{9,8},{10,11... | collective-permute-start | bytes 1585160 | tf_op jit(solution)/shard_map/ppermute | solution.py:351
  22.8 16.1 %collective-permute-start.4 = (bf16[1032,256]{1,0:T(8,128)(2,1)S(1)}, bf16[1032,256]{1,0:T(8,128)(2,1)S(1)}, u32[]{:S(2)}, u32[]{:S(2)}) collective-permute-start(bf16[1032,256]{1,0:T(8,128)(2,1)S(1)} %shard_map.86), channel_id=1, source_target_pairs={{0,1},{1,0},{2,3},{3,2},{4,5},{5,4},{6,7},{7,6},{8,9},{9,8},{10,11... | collective-permute-start | bytes 1585160 | tf_op jit(solution)/shard_map/ppermute | solution.py:351
  23.6 7.7 %collective-permute-start.9 = (bf16[264,256]{1,0:T(8,128)(2,1)S(1)}, bf16[264,256]{1,0:T(8,128)(2,1)S(1)}, u32[]{:S(2)}, u32[]{:S(2)}) collective-permute-start(bf16[264,256]{1,0:T(8,128)(2,1)S(1)} %get-tuple-element.34), channel_id=1, source_target_pairs={{0,2},{1,3},{2,0},{3,1},{4,6},{5,7},{6,4},{7,5},{8,10},{9,11},{10,... | collective-permute-start | bytes 405512 | tf_op jit(solution)/shard_map/ppermute | solution.py:351
  27.1 10.4 %collective-permute-start.10 = (bf16[264,256]{1,0:T(8,128)(2,1)S(1)}, bf16[264,256]{1,0:T(8,128)(2,1)S(1)}, u32[]{:S(2)}, u32[]{:S(2)}) collective-permute-start(bf16[264,256]{1,0:T(8,128)(2,1)S(1)} %get-tuple-element.35), channel_id=1, source_target_pairs={{0,4},{1,5},{2,6},{3,7},{4,0},{5,1},{6,2},{7,3},{8,12},{9,13},{10,... | collective-permute-start | bytes 405512 | tf_op jit(solution)/shard_map/ppermute | solution.py:351
  30.6 6.9 %collective-permute-start.11 = (bf16[264,256]{1,0:T(8,128)(2,1)S(1)}, bf16[264,256]{1,0:T(8,128)(2,1)S(1)}, u32[]{:S(2)}, u32[]{:S(2)}) collective-permute-start(bf16[264,256]{1,0:T(8,128)(2,1)S(1)} %get-tuple-element.36), channel_id=1, source_target_pairs={{0,6},{1,7},{2,4},{3,5},{4,2},{5,3},{6,0},{7,1},{8,14},{9,15},{10,... | collective-permute-start | bytes 405512 | tf_op jit(solution)/shard_map/ppermute | solution.py:351
  37.7 6.9 %collective-permute-start.12 = (bf16[264,256]{1,0:T(8,128)(2,1)S(1)}, bf16[264,256]{1,0:T(8,128)(2,1)S(1)}, u32[]{:S(2)}, u32[]{:S(2)}) collective-permute-start(bf16[264,256]{1,0:T(8,128)(2,1)S(1)} %shard_map.91), channel_id=1, source_target_pairs={{0,24},{8,16},{16,8},{24,0},{1,25},{9,17},{17,9},{25,1},{2,26},{10... | collective-permute-start | bytes 405512 | tf_op jit(solution)/shard_map/ppermute | solution.py:348
  39.1 6.1 %collective-permute-start.5 = (bf16[264,256]{1,0:T(8,128)(2,1)S(1)}, bf16[264,256]{1,0:T(8,128)(2,1)S(1)}, u32[]{:S(2)}, u32[]{:S(2)}) collective-permute-start(bf16[264,256]{1,0:T(8,128)(2,1)S(1)} %get-tuple-element.28), channel_id=1, source_target_pairs={{0,2},{1,3},{2,0},{3,1},{4,6},{5,7},{6,4},{7,5},{8,10},{9,11},{10,... | collective-permute-start | bytes 405512 | tf_op jit(solution)/shard_map/ppermute | solution.py:351
  40.3 7.7 %collective-permute-start.6 = (bf16[264,256]{1,0:T(8,128)(2,1)S(1)}, bf16[264,256]{1,0:T(8,128)(2,1)S(1)}, u32[]{:S(2)}, u32[]{:S(2)}) collective-permute-start(bf16[264,256]{1,0:T(8,128)(2,1)S(1)} %get-tuple-element.29), channel_id=1, source_target_pairs={{0,4},{1,5},{2,6},{3,7},{4,0},{5,1},{6,2},{7,3},{8,12},{9,13},{10,... | collective-permute-start | bytes 405512 | tf_op jit(solution)/shard_map/ppermute | solution.py:351
  41.5 6.5 %collective-permute-start.7 = (bf16[264,256]{1,0:T(8,128)(2,1)S(1)}, bf16[264,256]{1,0:T(8,128)(2,1)S(1)}, u32[]{:S(2)}, u32[]{:S(2)}) collective-permute-start(bf16[264,256]{1,0:T(8,128)(2,1)S(1)} %get-tuple-element.30), channel_id=1, source_target_pairs={{0,6},{1,7},{2,4},{3,5},{4,2},{5,3},{6,0},{7,1},{8,14},{9,15},{10,... | collective-permute-start | bytes 405512 | tf_op jit(solution)/shard_map/ppermute | solution.py:351

commit v3 on v2

--- a/solution.py
+++ b/solution.py
@@ -33,37 +33,61 @@
     return row[:, 0:1] + row[:, 1:2] * float(BASE) + row[:, 2:3] * float(BASE * BASE)
 
 
-def attention_kernel(
-    half, halves, groups, tile, extra,
-    len_h, own_h, emb_h, gout_h, wq_h, wk_h, wv_h, rows_h, *refs,
-):
-    outs = refs[:groups]
-    (emb, gout, wq, wk, wv, rows, len_ref, own_ref,
-     q_s, k_s, v_s, dq_s, dk_s, dv_s, tok_s, ext_s, idx_s, sems) = refs[groups:]
+def attention_kernel(half, halves, groups, tile, len_h, own_h, *refs):
+    first = half == 0
+    if first:
+        (emb_h, gout_h, wq_h, wk_h, wv_h, rows_h), refs = refs[:6], refs[6:]
+        outs, refs = refs[:groups], refs[groups:]
+        (wq, wk, wv, emb_next, gout_next, counts), refs = refs[:6], refs[6:]
+        (emb, gout, rows), refs = refs[:3], refs[3:]
+    else:
+        (emb, gout, wq, wk, wv, counts, kept), refs = refs[:7], refs[7:]
+        outs, refs = refs[:groups], refs[groups:]
+    len_ref, own_ref, q_s, k_s, v_s, dq_s, dk_s, dv_s, tok_s, ext_s, idx_s, sems = refs
     width = emb.shape[1]
     half_seqs = len_ref.shape[0] // halves
     half_tiles = own_ref.shape[0] // halves
-    span = emb.shape[0] // half_seqs
+    owned = half_tiles // groups
+    size = emb.shape[0]
+    span = size // half_seqs
     head = width // HEADS
     scale = 1.0 / math.sqrt(head)
     block = span // 2
-    start = half * half_seqs * span
-
-    def piece(s):
-        return pl.ds(s * span, span)
-
-    plan = [(len_h, len_ref)]
-    plan += [(emb_h.at[pl.ds(start, span)], emb.at[piece(0)]), (wq_h, wq), (wk_h, wk), (wv_h, wv)]
-    plan += [(gout_h.at[pl.ds(start, span)], gout.at[piece(0)])]
-    for s in range(1, half_seqs):
-        plan += [
-            (emb_h.at[pl.ds(start + s * span, span)], emb.at[piece(s)]),
-            (gout_h.at[pl.ds(start + s * span, span)], gout.at[piece(s)]),
+    sub = block // 2
+
+    def load(source, target, sem):
+        return pltpu.make_async_copy(source, target, sem)
+
+    def load_rows(source, target, base, at, count, sem):
+        return load(source.at[pl.ds(base + at, count)], target.at[pl.ds(at, count)], sem)
+
+    wait_len, wait_own = load(len_h, len_ref, sems.at[0]), load(own_h, own_ref, sems.at[1])
+    if first:
+        wait_len.start()
+        head_loads = [load(wq_h, wq, sems.at[2]), load(wk_h, wk, sems.at[3])]
+        head_loads += [load(wv_h, wv, sems.at[4])]
+        wait_rows = load(rows_h, rows, sems.at[5])
+
+        def loads(s):
+            low = load_rows(emb_h, emb, 0, s * span, block, sems.at[8 + 3 * s])
+            high = load_rows(emb_h, emb, 0, s * span + block, block, sems.at[9 + 3 * s])
+            other = load_rows(gout_h, gout, 0, s * span, span, sems.at[10 + 3 * s])
+            return low, high, other
+
+        for s in range(half_seqs):
+            low, high, other = loads(s)
+            low.start()
+            if s == 0:
+                for c in head_loads:
+                    c.start()
+            high.start()
+            other.start()
+        wait_rows.start()
+        later = [
+            load_rows(emb_h, emb_next, size, 0, size, sems.at[6]),
+            load_rows(gout_h, gout_next, size, 0, size, sems.at[7]),
         ]
-    plan += [(own_h, own_ref), (rows_h, rows)]
-    copies = [pltpu.make_async_copy(a, b, sems.at[i]) for i, (a, b) in enumerate(plan)]
-    for c in copies:
-        c.start()
+    wait_own.start()
 
     def gate(raw, grad, weight):
         grown = jnp.exp(raw * (-scale))
@@ -75,40 +99,60 @@
             (grad * weight * slope).astype(jnp.bfloat16),
         )
 
+    def project(base, at):
+        rows_in = emb[pl.ds(base + at, block), :]
+        q_s[at:at + block, :] = dot(rows_in, wq[...]).astype(jnp.bfloat16)
+        k_s[at:at + block, :] = dot(rows_in, wk[...]).astype(jnp.bfloat16)
+        v_s[at:at + block, :] = dot(rows_in, wv[...]).astype(jnp.bfloat16)
+
     def run(base, count, live):
-        def rows_of(ref, at, size):
-            return ref[base + at:base + at + size, :]
-
-        q_s[0:live, :] = dot(rows_of(emb, 0, live), wq[...]).astype(jnp.bfloat16)
-        k_s[0:live, :] = dot(rows_of(emb, 0, live), wk[...]).astype(jnp.bfloat16)
-        v_s[0:live, :] = dot(rows_of(emb, 0, live), wv[...]).astype(jnp.bfloat16)
+        if live > block:
+            project(base, block)
         lane = lax.broadcasted_iota(jnp.int32, (1, block), 1)
         inverse = 1.0 / jnp.broadcast_to(count, (1, block)).astype(jnp.float32)
-        sub = lax.broadcasted_iota(jnp.int32, (block, block), 0)
-        lan = lax.broadcasted_iota(jnp.int32, (block, block), 1)
-        causal = sub <= lan
+        causal = lax.broadcasted_iota(jnp.int32, (sub, sub), 0) <= lax.broadcasted_iota(
+            jnp.int32, (sub, sub), 1
+        )
+        zeros = jnp.zeros((sub, sub), jnp.bfloat16)
         for h in range(HEADS):
             cols = slice(h * head, (h + 1) * head)
             att, sco = {}, {}
             for i in range(live // block):
                 weight = jnp.where(lane + i * block < count, inverse, 0.0)
                 iq = q_s[i * block:(i + 1) * block, cols]
-                ig = gout[base + i * block:base + (i + 1) * block, cols]
+                ig = gout[pl.ds(base + i * block, block), cols]
                 for j in range(i + 1):
                     jk = k_s[j * block:(j + 1) * block, cols]
                     jv = v_s[j * block:(j + 1) * block, cols]
                     raw = dot(jk, iq, NT)
                     grad = dot(jv, ig, NT)
-                    if i == j:
-                        use = jnp.where(causal, weight, 0.0)
-                    else:
-                        use = weight
-                    att[j, i], sco[j, i] = gate(raw, grad, use)
+                    if i != j:
+                        att[j, i], sco[j, i] = gate(raw, grad, weight)
+                        continue
+                    low, high = weight[:, :sub], weight[:, sub:]
+                    a0, s0 = gate(
+                        raw[:sub, :sub], grad[:sub, :sub], jnp.where(causal, low, 0.0)
+                    )
+                    a1, s1 = gate(raw[:sub, sub:], grad[:sub, sub:], high)
+                    a2, s2 = gate(
+                        raw[sub:, sub:], grad[sub:, sub:], jnp.where(causal, high, 0.0)
+                    )
+
+                    def whole(x, y, z):
+                        return jnp.concatenate(
+                            [
+                                jnp.concatenate([x, y], axis=1),
+                                jnp.concatenate([zeros, z], axis=1),
+                            ],
+                            axis=0,
+                        )
+
+                    att[j, i], sco[j, i] = whole(a0, a1, a2), whole(s0, s1, s2)
             for j in range(live // block):
                 vg = kg = None
                 for i in range(j, live // block):
                     iq = q_s[i * block:(i + 1) * block, cols]
-                    ig = gout[base + i * block:base + (i + 1) * block, cols]
+                    ig = gout[pl.ds(base + i * block, block), cols]
                     a, b = dot(att[j, i], ig), dot(sco[j, i], iq)
                     vg = a if vg is None else vg + a
                     kg = b if kg is None else kg + b
@@ -124,24 +168,44 @@
         token = dot(dq_s[0:live, :], wq[...], NT)
         token = token + dot(dk_s[0:live, :], wk[...], NT)
         token = token + dot(dv_s[0:live, :], wv[...], NT)
-        tok_s[base:base + live, :] = token.astype(jnp.bfloat16)
+        tok_s[pl.ds(base, live), :] = token.astype(jnp.bfloat16)
         if live < span:
-            tok_s[base + live:base + span, :] = jnp.zeros((span - live, width), jnp.bfloat16)
-
-    for c in copies[:6]:
-        c.wait()
-    for s in range(half_seqs):
-        if s:
-            for c in copies[4 + 2 * s:6 + 2 * s]:
-                c.wait()
-        count = len_ref[half * half_seqs + s]
-        pl.when(count <= block)(functools.partial(run, s * span, count, block))
-        pl.when(count > block)(functools.partial(run, s * span, count, span))
-    for c in copies[-2:]:
-        c.wait()
+            tok_s[pl.ds(base + live, span - live), :] = jnp.zeros((span - live, width), jnp.bfloat16)
+
+    if first:
+        for c in head_loads:
+            c.wait()
+        wait_len.wait()
+        for s in range(len_ref.shape[0]):
+            counts[s:s + 1, :] = jnp.broadcast_to(len_ref[s], (1, counts.shape[1]))
+
+    def one(s, carry):
+        base = pl.multiple_of(s * span, span)
+        if first:
+            low, high, other = loads(s)
+            low.wait()
+        project(base, 0)
+        if first:
+            high.wait()
+            other.wait()
+
+            @pl.when(s == half_seqs - 1)
+            def _():
+                for c in later:
+                    c.start()
+
+        if first:
+            count = len_ref[half * half_seqs + s]
+        else:
+            count = jnp.max(counts[pl.ds(half * half_seqs + s, 1), :])
+        pl.when(count <= block)(functools.partial(run, base, count, block))
+        pl.when(count > block)(functools.partial(run, base, count, span))
+        return carry
+
+    lax.fori_loop(0, half_seqs, one, 0)
+    wait_own.wait()
 
     me = lax.axis_index("group")
-    owned = half_tiles // groups
 
     def place(part):
         for g in range(groups):
@@ -152,14 +216,15 @@
             idx_s[owner * owned + seen] = t
             idx_s[groups * owned + owner] = seen + 1
 
-    if extra:
+    if first:
+        wait_rows.wait()
         total = len_ref[0]
         for s in range(1, len_ref.shape[0]):
             total = total + len_ref[s]
         for k in range(groups):
             ext_s[k] = jnp.zeros(ext_s.shape[1:], jnp.float32)
             ext_s[k, halves * owned:halves * owned + 1, :] = digits_row(total, width)
-        for part in range(halves):
+        for part in range(halves - 1, -1, -1):
             place(part)
             for k in range(groups):
                 owner = me ^ k
@@ -171,53 +236,69 @@
                     ext_s[k, at:at + 1, tile:2 * tile] = (row % ROWS_DEV).astype(jnp.float32)
         for k in range(groups):
             outs[k][owned * tile:owned * tile + EXTRA, :] = ext_s[k].astype(jnp.bfloat16)
-    place(half)
+    else:
+        place(half)
     for k in range(groups):
         owner = me ^ k
+        shift = 0
+        if not first and k == groups - 1:
+            shift = owned * tile
+            outs[k][0:shift, :] = kept[0:shift, :]
+            outs[k][2 * shift:2 * shift + EXTRA, :] = kept[shift:shift + EXTRA, :]
         for s in range(owned):
             t = idx_s[owner * owned + s]
-            outs[k][s * tile:(s + 1) * tile, :] = tok_s[
+            outs[k][shift + s * tile:shift + (s + 1) * tile, :] = tok_s[
                 pl.ds(pl.multiple_of(t * tile, tile), tile), :
             ]
-
-
-def attention(half, halves, groups, lengths, owners, embeds, out_grad, wq, wk, wv, rows, extra):
-    tokens, width = embeds.shape
-    seqs = lengths.shape[0]
-    span = tokens // seqs
-    tile = tokens // owners.shape[0]
-    half_seqs, half_tiles = seqs // halves, owners.shape[0] // halves
+    if first:
+        for c in later:
+            c.wait()
+
+
+def attention(half, halves, groups, lengths, owners, *given):
+    width = given[0].shape[1]
+    first = half == 0
+    size = given[0].shape[0] // (halves if first else 1)
+    seqs, tiles = lengths.shape[0], owners.shape[0]
+    span = size * halves // seqs
+    tile = size * halves // tiles
+    half_seqs, half_tiles = seqs // halves, tiles // halves
     owned = half_tiles // groups
-    out_rows = owned * tile + (EXTRA if extra else 0)
+    bf16 = jnp.bfloat16
+    box = owned * tile
     flops = half_seqs * (2 * span * width * width * 6 + 10 * span * span * width)
-    bf16 = jnp.bfloat16
-    return pl.pallas_call(
-        functools.partial(attention_kernel, half, halves, groups, tile, extra),
-        in_specs=[pl.BlockSpec(memory_space=pltpu.HBM)] * 8,
-        out_specs=vmem(groups),
-        out_shape=[jax.ShapeDtypeStruct((out_rows, width), bf16)] * groups,
-        scratch_shapes=[pltpu.VMEM((half_seqs * span, width), bf16)] * 2
-        + [pltpu.VMEM((width, width), bf16)] * 3
-        + [
-            pltpu.VMEM(rows.shape, jnp.int32),
-            pltpu.SMEM(lengths.shape, jnp.int32),
-            pltpu.SMEM(owners.shape, jnp.int32),
-        ]
+    hbm = pl.BlockSpec(memory_space=pltpu.HBM)
+    scratch = []
+    if first:
+        given = [pltpu.with_memory_space_constraint(a, pltpu.HBM) for a in given]
+        specs = [hbm] * len(given)
+        shapes = [(box + EXTRA, width)] * groups + [(width, width)] * 3 + [(size, width)] * 2
+        shapes = [(s, bf16) for s in shapes] + [((EXTRA, 128), jnp.int32)]
+        scratch = [pltpu.VMEM((size, width), bf16)] * 2 + [pltpu.VMEM((tiles, tile), jnp.int32)]
+    else:
+        specs = vmem(len(given))
+        shapes = [(box, width)] * (groups - 1) + [(2 * box + EXTRA, width)]
+        shapes = [(s, bf16) for s in shapes]
+    small = [pltpu.with_memory_space_constraint(a, pltpu.HBM) for a in (lengths, owners)]
+    return list(pl.pallas_call(
+        functools.partial(attention_kernel, half, halves, groups, tile),
+        in_specs=[hbm, hbm] + specs,
+        out_specs=vmem(len(shapes)),
+        out_shape=[jax.ShapeDtypeStruct(s, d) for s, d in shapes],
+        scratch_shapes=scratch
+        + [pltpu.SMEM(lengths.shape, jnp.int32), pltpu.SMEM(owners.shape, jnp.int32)]
         + [pltpu.VMEM((span, width), bf16)] * 6
         + [
             pltpu.VMEM((half_seqs * span, width), bf16),
             pltpu.VMEM((groups, EXTRA, width), jnp.float32),
             pltpu.SMEM((groups * owned + groups,), jnp.int32),
-            pltpu.SemaphoreType.DMA((6 + 2 * half_seqs,)),
+            pltpu.SemaphoreType.DMA((8 + 3 * half_seqs,)),
         ],
         compiler_params=pltpu.CompilerParams(vmem_limit_bytes=LIMIT),
         cost_estimate=pl.CostEstimate(
             flops=flops, bytes_accessed=4 * half_seqs * span * width * 2, transcendentals=0
         ),
-    )(*[
-        pltpu.with_memory_space_constraint(a, pltpu.HBM)
-        for a in (lengths, owners, embeds, out_grad, wq, wk, wv, rows)
-    ])
+    )(*small, *given))
 
 
 def sums_of(block, boxes, exts, first, owned, tile):
@@ -294,6 +375,18 @@
         outs[k][ROWS_DEV:ROWS_DEV + EXTRA, :] = live_rows(live, outs[k])
 
 
+def far_pair_kernel(pairs, slots, tile, *refs):
+    boxes, outs = refs[:2], refs[2:]
+    core, pair = lax.axis_index("batch") % 2, lax.axis_index("batch") // 2
+    exts = exts_of(boxes, slots * tile)
+    live = live_of(exts, slots)
+    for k in range(pairs):
+        block = 2 * (pair ^ k) + core
+        total = sums_of(block, boxes, exts, 0, slots, tile)
+        outs[k][0:ROWS_DEV, :] = total.astype(outs[k].dtype)
+        outs[k][ROWS_DEV:ROWS_DEV + EXTRA, :] = live_rows(live, outs[k])
+
+
 def gathered(ins):
     total = live = None
     for r in ins:
@@ -350,14 +443,19 @@
     def across(box, k):
         return lax.ppermute(box, "batch", [(i, i ^ k) for i in range(batches)])
 
-    near, away = [], []
+    near = []
+    mine = attention(
+        0, halves, groups, lengths, tile_owner, embeds, out_grad, w_query, w_key, w_value, rows
+    )
+    w_all, (emb_next, gout_next) = mine[groups:groups + 3], mine[groups + 3:groups + 5]
+    counts = mine[-1]
     for half in range(halves):
-        mine = list(attention(
-            half, halves, groups, lengths, tile_owner, embeds, out_grad,
-            w_query, w_key, w_value, rows, half == 0,
-        ))
+        if half:
+            mine = attention(
+                half, halves, groups, lengths, tile_owner, emb_next, gout_next, *w_all, counts, mine[far]
+            )
         near.append([mine[0]] + [swap(mine[k], k) for k in range(far - 1, 0, -1)])
-        away.append([mine[far]])
+    away = mine[far]
 
     def side(which, flops, heads, bodies, acc=None):
         out = shape((pairs * ROWS_DEV + EXTRA, width), bf16) if which == 0 else shape(
@@ -395,7 +493,12 @@
         )
         return [parts[0]] + [across(parts[k], 2 * k) for k in range(1, pairs)]
 
-    far_parts = plane(away[0], away[1])
+    far_parts = call(
+        functools.partial(far_pair_kernel, pairs, halves * owned, tile),
+        [shape((ROWS_DEV + EXTRA, width), f32 if k == 0 else bf16) for k in range(pairs)],
+        4 * work, away, across(away, 1),
+    )
+    far_parts = [far_parts[0]] + [across(far_parts[k], 2 * k) for k in range(1, pairs)]
     acc = call(
         functools.partial(first_kernel, pairs, owned, tile),
         shape((2, pairs, ROWS_DEV, width), f32), 2 * far * work, *near[0],

time: 49 us -> 49.4 us (level)
  waiting for transfers between devices: 17.8 us -> 19.6 us
  Pallas kernels: 12.7 us -> 10.9 us
  starting transfers between devices: 18.2 us -> 18.7 us
    ppermute x8, waiting for transfers between devices: 9.73 us -> 11.3 us  [across(): return lax.ppermute(box, 'batch', [(i, i ^ k) for i in range(batches)])]
    pallas_call x2, Pallas kernels: 8.17 us -> 6.77 us  [attention(): pl.pallas_call(functools.partial(attention_kernel, half, halves, groups,...]
    pallas_call x4 -> x2, Pallas kernels: 2.01 us -> 1.15 us  [side(): pl.pallas_call(functools.partial(side_kernel, which, pairs, owned, tile,...]
    ppermute x5, starting transfers between devices: 7.53 us -> 8.03 us  [swap(): return lax.ppermute(box, 'group', [(i, i ^ k) for i in range(groups)])]
  transfers between devices with their start and end apart: 13 -> 13, of which waited for: 6 -> 9; matrix products, arithmetic and copies ran while one was open for 0% -> 0% of each run, Pallas kernels for 16% -> 11%
where the time goes in v3:
time: 49.4 us; the launch traced here: 49.3 us
  waiting for transfers between devices  19.6 us (40%)
  starting transfers between devices  18.7 us (38%)
  Pallas kernels  10.9 us (22%)
    ppermute x8, waiting for transfers between devices, across(): return lax.ppermute(box, 'batch', [(i, i ^ k) for i in range(batches)])  11.3 us
    ppermute x8, starting transfers between devices, across(): return lax.ppermute(box, 'batch', [(i, i ^ k) for i in range(batches)])  10.7 us
    ppermute x5, waiting for transfers between devices, swap(): return lax.ppermute(box, 'group', [(i, i ^ k) for i in range(groups)])  8.26 us
    ppermute x5, starting transfers between devices, swap(): return lax.ppermute(box, 'group', [(i, i ^ k) for i in range(groups)])  8.03 us
    pallas_call x2, Pallas kernels, attention(): pl.pallas_call(functools.partial(attention_kernel, half, halves, groups,...  6.77 us
    pallas_call x5, Pallas kernels, call(): pl.pallas_call(kernel, in_specs=vmem(len(args)), out_specs=vmem(len(shape...  3.03 us
    pallas_call x2, Pallas kernels, side(): pl.pallas_call(functools.partial(side_kernel, which, pairs, owned, tile,...  1.15 us
  transfers between devices with their start and end apart: 13, of which 9 were waited for; matrix products, arithmetic and copies ran while one was open for 0% of the time, Pallas kernels for 11%

profile of v3, /device:TPU:0, one launch (start us, length us, event | category | flops | bytes accessed | tf_op | source)
XLA Modules:
  0.0 49.3 jit_solution(11959396104700413450)
XLA Ops:
  0.0 4.0 %shard_map.82 = (bf16[264,256]{1,0:T(8,128)(2,1)S(1)}, bf16[264,256]{1,0:T(8,128)(2,1)S(1)}, bf16[264,256]{1,0:T(8,128)(2,1)S(1)}, bf16[264,256]{1,0:T(8,128)(2,...) custom-call(s32[4]{0:T(128)} %len_h.3, s32[16]{0:T(128)} %own_h.3, ...), custom_call_target="tpu_custom_call" | custom-call | flops 2147483648 | bytes 2097152 | tf_op jit(solution)/shard_map/pallas_call | solution.py:283
  4.0 4.1 %collective-permute-start = (bf16[264,256]{1,0:T(8,128)(2,1)S(1)}, bf16[264,256]{1,0:T(8,128)(2,1)S(1)}, u32[]{:S(2)}, u32[]{:S(2)}) collective-permute-start(bf16[264,256]{1,0:T(8,128)(2,1)S(1)} %get-tuple-element.28), channel_id=1, source_target_pairs={{0,16},{8,24},{16,0},{24,8},{1,17},{9,25},{17,1},{25,9},{2,18},{10... | collective-permute-start | bytes 405512 | tf_op jit(solution)/shard_map/ppermute | solution.py:441
  8.1 1.6 %collective-permute-start.1 = (bf16[264,256]{1,0:T(8,128)(2,1)S(1)}, bf16[264,256]{1,0:T(8,128)(2,1)S(1)}, u32[]{:S(2)}, u32[]{:S(2)}) collective-permute-start(bf16[264,256]{1,0:T(8,128)(2,1)S(1)} %get-tuple-element.29), channel_id=1, source_target_pairs={{0,8},{8,0},{16,24},{24,16},{1,9},{9,1},{17,25},{25,17},{2,10},{10... | collective-permute-start | bytes 405512 | tf_op jit(solution)/shard_map/ppermute | solution.py:441
  9.7 2.8 %shard_map.83 = (bf16[256,256]{1,0:T(8,128)(2,1)S(1)}, bf16[256,256]{1,0:T(8,128)(2,1)S(1)}, bf16[256,256]{1,0:T(8,128)(2,1)S(1)}, bf16[520,256]{1,0:T(8,128)(2,1)S(1)}) custom-call(s32[4]{0:T(128)} %len_h.3, s32[16]{0:T(128)} %own_h.3, bf16[1024,256]{1,0:T(8,128)(2,1)S(1)} %get-tuple-element.30.refs_0_, bf16[1024,256]{1,0:T(8,128)(2,1)S(1)} %get-tuple-element.31.refs_1_, ...), custom_call_target="tpu_custom_call" | custom-call | flops 2147483648 | bytes 2097152 | tf_op jit(solution)/shard_map/pallas_call | solution.py:283
  12.5 0.4 collective-permute-start.2
  12.9 0.2 collective-permute-start.3
  13.1 1.6 %collective-permute-done.refs_1_ = bf16[264,256]{1,0:T(8,128)(2,1)S(1)} collective-permute-done((bf16[264,256]{1,0:T(8,128)(2,1)S(1)}, bf16[264,256]{1,0:T(8,128)(2,1)S(1)}, u32[]{:S(2)}, u32[]{:S(2)}) %collective-permute-start) | collective-permute-done | bytes 135200 | tf_op jit(solution)/shard_map/ppermute | solution.py:441
  14.7 0.4 collective-permute-done.1.refs_2_
  15.1 1.0 %shard_map.84.refs_6_ = f32[2,4,256,256]{3,2,1,0:T(8,128)S(1)} custom-call(bf16[264,256]{1,0:T(8,128)(2,1)S(1)} %get-tuple-element.27.refs_0_, bf16[264,256]{1,0:T(8,128)(2,1)S(1)} %collective-permute-done.refs_1_, bf16[264,256]{1,0:T(8,128)(2,1)S(1)} %collective-permute-done.1.refs_2_), custom_call_target="tpu_custom_call" | custom-call | flops 805306368 | bytes 1048576 | tf_op jit(solution)/shard_map/pallas_call | solution.py:417
  16.1 4.8 %collective-permute-done.2.refs_4_ = bf16[256,256]{1,0:T(8,128)(2,1)S(1)} collective-permute-done((bf16[256,256]{1,0:T(8,128)(2,1)S(1)}, bf16[256,256]{1,0:T(8,128)(2,1)S(1)}, u32[]{:S(2)}, u32[]{:S(2)}) %collective-permute-start.2) | collective-permute-done | bytes 131104 | tf_op jit(solution)/shard_map/ppermute | solution.py:441
  20.9 0.0 collective-permute-done.3.refs_5_
  20.9 0.6 %shard_map.86 = bf16[1032,256]{1,0:T(8,128)(2,1)S(1)} custom-call(bf16[264,256]{1,0:T(8,128)(2,1)S(1)} %get-tuple-element.27.refs_0_, bf16[264,256]{1,0:T(8,128)(2,1)S(1)} %collective-permute-done.refs_1_, bf16[264,256]{1,0:T(8,128)(2,1)S(1)} %collective-permute-done.1.refs_2_, bf16[256,256]{1,0:T(8,128)(2,1)S(1)} %get-tuple-element.37.refs_3_, ...), custom_call_target="tpu_custom_call" | custom-call | flops 402653184 | bytes 1048576 | tf_op jit(solution)/shard_map/pallas_call | solution.py:470
  21.5 0.1 collective-permute-start.4
  21.5 0.5 %collective-permute-start.8 = (bf16[520,256]{1,0:T(8,128)(2,1)S(1)}, bf16[520,256]{1,0:T(8,128)(2,1)S(1)}, u32[]{:S(2)}, u32[]{:S(2)}) collective-permute-start(bf16[520,256]{1,0:T(8,128)(2,1)S(1)} %get-tuple-element.44.refs_0_), channel_id=1, source_target_pairs={{0,1},{1,0},{2,3},{3,2},{4,5},{5,4},{6,7},{7,6},{8,9},{9,8},{10,11... | collective-permute-start | bytes 798728 | tf_op jit(solution)/shard_map/ppermute | solution.py:444
  22.0 1.8 %collective-permute-done.8.refs_1_ = bf16[520,256]{1,0:T(8,128)(2,1)S(1)} collective-permute-done((bf16[520,256]{1,0:T(8,128)(2,1)S(1)}, bf16[520,256]{1,0:T(8,128)(2,1)S(1)}, u32[]{:S(2)}, u32[]{:S(2)}) %collective-permute-start.8) | collective-permute-done | bytes 266272 | tf_op jit(solution)/shard_map/ppermute | solution.py:444
  23.8 0.7 %shard_map.88 = (f32[264,256]{1,0:T(8,128)S(1)}, bf16[264,256]{1,0:T(8,128)(2,1)S(1)}, bf16[264,256]{1,0:T(8,128)(2,1)S(1)}, bf16[264,256]{1,0:T(8,128)(2,1)S(1)}) custom-call(bf16[520,256]{1,0:T(8,128)(2,1)S(1)} %get-tuple-element.44.refs_0_, bf16[520,256]{1,0:T(8,128)(2,1)S(1)} %collective-permute-done.8.refs_1_), custom_call_target="tpu_custom_call" | custom-call | flops 536870912 | bytes 1048576 | tf_op jit(solution)/shard_map/pallas_call | solution.py:417
  24.5 3.4 %collective-permute-start.9 = (bf16[264,256]{1,0:T(8,128)(2,1)S(1)}, bf16[264,256]{1,0:T(8,128)(2,1)S(1)}, u32[]{:S(2)}, u32[]{:S(2)}) collective-permute-start(bf16[264,256]{1,0:T(8,128)(2,1)S(1)} %get-tuple-element.46), channel_id=1, source_target_pairs={{0,2},{1,3},{2,0},{3,1},{4,6},{5,7},{6,4},{7,5},{8,10},{9,11},{10,... | collective-permute-start | bytes 405512 | tf_op jit(solution)/shard_map/ppermute | solution.py:444
  27.9 3.2 %collective-permute-start.10 = (bf16[264,256]{1,0:T(8,128)(2,1)S(1)}, bf16[264,256]{1,0:T(8,128)(2,1)S(1)}, u32[]{:S(2)}, u32[]{:S(2)}) collective-permute-start(bf16[264,256]{1,0:T(8,128)(2,1)S(1)} %get-tuple-element.47), channel_id=1, source_target_pairs={{0,4},{1,5},{2,6},{3,7},{4,0},{5,1},{6,2},{7,3},{8,12},{9,13},{10,... | collective-permute-start | bytes 405512 | tf_op jit(solution)/shard_map/ppermute | solution.py:444
  31.1 0.0 collective-permute-start.11
  31.1 0.6 %shard_map.85.refs_3_ = f32[1024,256]{1,0:T(8,128)S(1)} custom-call(bf16[264,256]{1,0:T(8,128)(2,1)S(1)} %get-tuple-element.27.refs_0_, bf16[264,256]{1,0:T(8,128)(2,1)S(1)} %collective-permute-done.refs_1_, bf16[264,256]{1,0:T(8,128)(2,1)S(1)} %collective-permute-done.1.refs_2_, bf16[256,256]{1,0:T(8,128)(2,1)S(1)} %get-tuple-element.37.refs_3_, ...), custom_call_target="tpu_custom_call" | custom-call | flops 402653184 | bytes 1048576 | tf_op jit(solution)/shard_map/pallas_call | solution.py:470
  31.6 0.1 collective-permute-done.9.refs_1_
  31.8 5.8 %collective-permute-done.10.refs_2_ = bf16[264,256]{1,0:T(8,128)(2,1)S(1)} collective-permute-done((bf16[264,256]{1,0:T(8,128)(2,1)S(1)}, bf16[264,256]{1,0:T(8,128)(2,1)S(1)}, u32[]{:S(2)}, u32[]{:S(2)}) %collective-permute-start.10) | collective-permute-done | bytes 135200 | tf_op jit(solution)/shard_map/ppermute | solution.py:444
  37.6 0.0 collective-permute-done.11.refs_3_
  37.6 0.2 shard_map.89
  37.8 1.7 %collective-permute-start.12 = (bf16[264,256]{1,0:T(8,128)(2,1)S(1)}, bf16[264,256]{1,0:T(8,128)(2,1)S(1)}, u32[]{:S(2)}, u32[]{:S(2)}) collective-permute-start(bf16[264,256]{1,0:T(8,128)(2,1)S(1)} %shard_map.89), channel_id=1, source_target_pairs={{0,24},{8,16},{16,8},{24,0},{1,25},{9,17},{17,9},{25,1},{2,26},{10... | collective-permute-start | bytes 405512 | tf_op jit(solution)/shard_map/ppermute | solution.py:441
  39.5 0.0 collective-permute-done.4.refs_4_
  39.5 0.2 shard_map.87
  39.8 1.5 %collective-permute-start.5 = (bf16[264,256]{1,0:T(8,128)(2,1)S(1)}, bf16[264,256]{1,0:T(8,128)(2,1)S(1)}, u32[]{:S(2)}, u32[]{:S(2)}) collective-permute-start(bf16[264,256]{1,0:T(8,128)(2,1)S(1)} %get-tuple-element.41), channel_id=1, source_target_pairs={{0,2},{1,3},{2,0},{3,1},{4,6},{5,7},{6,4},{7,5},{8,10},{9,11},{10,... | collective-permute-start | bytes 405512 | tf_op jit(solution)/shard_map/ppermute | solution.py:444
  41.3 0.6 %collective-permute-start.6 = (bf16[264,256]{1,0:T(8,128)(2,1)S(1)}, bf16[264,256]{1,0:T(8,128)(2,1)S(1)}, u32[]{:S(2)}, u32[]{:S(2)}) collective-permute-start(bf16[264,256]{1,0:T(8,128)(2,1)S(1)} %get-tuple-element.42), channel_id=1, source_target_pairs={{0,4},{1,5},{2,6},{3,7},{4,0},{5,1},{6,2},{7,3},{8,12},{9,13},{10,... | collective-permute-start | bytes 405512 | tf_op jit(solution)/shard_map/ppermute | solution.py:444
  41.9 1.4 %collective-permute-start.7 = (bf16[264,256]{1,0:T(8,128)(2,1)S(1)}, bf16[264,256]{1,0:T(8,128)(2,1)S(1)}, u32[]{:S(2)}, u32[]{:S(2)}) collective-permute-start(bf16[264,256]{1,0:T(8,128)(2,1)S(1)} %get-tuple-element.43), channel_id=1, source_target_pairs={{0,6},{1,7},{2,4},{3,5},{4,2},{5,3},{6,0},{7,1},{8,14},{9,15},{10,... | collective-permute-start | bytes 405512 | tf_op jit(solution)/shard_map/ppermute | solution.py:444
  43.3 1.5 %collective-permute-done.12.refs_4_ = bf16[264,256]{1,0:T(8,128)(2,1)S(1)} collective-permute-done((bf16[264,256]{1,0:T(8,128)(2,1)S(1)}, bf16[264,256]{1,0:T(8,128)(2,1)S(1)}, u32[]{:S(2)}, u32[]{:S(2)}) %collective-permute-start.12) | collective-permute-done | bytes 135200 | tf_op jit(solution)/shard_map/ppermute | solution.py:441
  44.8 1.1 %collective-permute-done.5.refs_1_ = bf16[264,256]{1,0:T(8,128)(2,1)S(1)} collective-permute-done((bf16[264,256]{1,0:T(8,128)(2,1)S(1)}, bf16[264,256]{1,0:T(8,128)(2,1)S(1)}, u32[]{:S(2)}, u32[]{:S(2)}) %collective-permute-start.5) | collective-permute-done | bytes 135200 | tf_op jit(solution)/shard_map/ppermute | solution.py:444
  45.9 2.5 %collective-permute-done.6.refs_2_ = bf16[264,256]{1,0:T(8,128)(2,1)S(1)} collective-permute-done((bf16[264,256]{1,0:T(8,128)(2,1)S(1)}, bf16[264,256]{1,0:T(8,128)(2,1)S(1)}, u32[]{:S(2)}, u32[]{:S(2)}) %collective-permute-start.6) | collective-permute-done | bytes 135200 | tf_op jit(solution)/shard_map/ppermute | solution.py:444
  48.4 0.0 collective-permute-done.7.refs_3_
  48.4 0.9 %shard_map.90 = f32[256,256]{1,0:T(8,128)} custom-call(f32[264,256]{1,0:T(8,128)S(1)} %get-tuple-element.40.refs_0_, bf16[264,256]{1,0:T(8,128)(2,1)S(1)} %collective-permute-done.5.refs_1_, bf16[264,256]{1,0:T(8,128)(2,1)S(1)} %collective-permute-done.6.refs_2_, bf16[264,256]{1,0:T(8,128)(2,1)S(1)} %collective-permute-done.7.refs_3_, ...), custom_call_target="tpu_custom_call" | custom-call | flops 1048576 | bytes 1048576 | tf_op jit(solution)/shard_map/pallas_call | solution.py:417
Async XLA Ops:
  4.0 10.7 %collective-permute-start = (bf16[264,256]{1,0:T(8,128)(2,1)S(1)}, bf16[264,256]{1,0:T(8,128)(2,1)S(1)}, u32[]{:S(2)}, u32[]{:S(2)}) collective-permute-start(bf16[264,256]{1,0:T(8,128)(2,1)S(1)} %get-tuple-element.28), channel_id=1, source_target_pairs={{0,16},{8,24},{16,0},{24,8},{1,17},{9,25},{17,1},{25,9},{2,18},{10... | collective-permute-start | bytes 405512 | tf_op jit(solution)/shard_map/ppermute | solution.py:441
  8.1 6.9 %collective-permute-start.1 = (bf16[264,256]{1,0:T(8,128)(2,1)S(1)}, bf16[264,256]{1,0:T(8,128)(2,1)S(1)}, u32[]{:S(2)}, u32[]{:S(2)}) collective-permute-start(bf16[264,256]{1,0:T(8,128)(2,1)S(1)} %get-tuple-element.29), channel_id=1, source_target_pairs={{0,8},{8,0},{16,24},{24,16},{1,9},{9,1},{17,25},{25,17},{2,10},{10... | collective-permute-start | bytes 405512 | tf_op jit(solution)/shard_map/ppermute | solution.py:441
  12.5 8.4 %collective-permute-start.2 = (bf16[256,256]{1,0:T(8,128)(2,1)S(1)}, bf16[256,256]{1,0:T(8,128)(2,1)S(1)}, u32[]{:S(2)}, u32[]{:S(2)}) collective-permute-start(bf16[256,256]{1,0:T(8,128)(2,1)S(1)} %get-tuple-element.38), channel_id=1, source_target_pairs={{0,16},{8,24},{16,0},{24,8},{1,17},{9,25},{17,1},{25,9},{2,18},{10... | collective-permute-start | bytes 393224 | tf_op jit(solution)/shard_map/ppermute | solution.py:441
  12.9 8.0 %collective-permute-start.3 = (bf16[256,256]{1,0:T(8,128)(2,1)S(1)}, bf16[256,256]{1,0:T(8,128)(2,1)S(1)}, u32[]{:S(2)}, u32[]{:S(2)}) collective-permute-start(bf16[256,256]{1,0:T(8,128)(2,1)S(1)} %get-tuple-element.39), channel_id=1, source_target_pairs={{0,8},{8,0},{16,24},{24,16},{1,9},{9,1},{17,25},{25,17},{2,10},{10... | collective-permute-start | bytes 393224 | tf_op jit(solution)/shard_map/ppermute | solution.py:441
  21.5 18.1 %collective-permute-start.4 = (bf16[1032,256]{1,0:T(8,128)(2,1)S(1)}, bf16[1032,256]{1,0:T(8,128)(2,1)S(1)}, u32[]{:S(2)}, u32[]{:S(2)}) collective-permute-start(bf16[1032,256]{1,0:T(8,128)(2,1)S(1)} %shard_map.86), channel_id=1, source_target_pairs={{0,1},{1,0},{2,3},{3,2},{4,5},{5,4},{6,7},{7,6},{8,9},{9,8},{10,11... | collective-permute-start | bytes 1585160 | tf_op jit(solution)/shard_map/ppermute | solution.py:444
  21.5 2.3 %collective-permute-start.8 = (bf16[520,256]{1,0:T(8,128)(2,1)S(1)}, bf16[520,256]{1,0:T(8,128)(2,1)S(1)}, u32[]{:S(2)}, u32[]{:S(2)}) collective-permute-start(bf16[520,256]{1,0:T(8,128)(2,1)S(1)} %get-tuple-element.44.refs_0_), channel_id=1, source_target_pairs={{0,1},{1,0},{2,3},{3,2},{4,5},{5,4},{6,7},{7,6},{8,9},{9,8},{10,11... | collective-permute-start | bytes 798728 | tf_op jit(solution)/shard_map/ppermute | solution.py:444
  24.5 7.3 %collective-permute-start.9 = (bf16[264,256]{1,0:T(8,128)(2,1)S(1)}, bf16[264,256]{1,0:T(8,128)(2,1)S(1)}, u32[]{:S(2)}, u32[]{:S(2)}) collective-permute-start(bf16[264,256]{1,0:T(8,128)(2,1)S(1)} %get-tuple-element.46), channel_id=1, source_target_pairs={{0,2},{1,3},{2,0},{3,1},{4,6},{5,7},{6,4},{7,5},{8,10},{9,11},{10,... | collective-permute-start | bytes 405512 | tf_op jit(solution)/shard_map/ppermute | solution.py:444
  27.9 9.7 %collective-permute-start.10 = (bf16[264,256]{1,0:T(8,128)(2,1)S(1)}, bf16[264,256]{1,0:T(8,128)(2,1)S(1)}, u32[]{:S(2)}, u32[]{:S(2)}) collective-permute-start(bf16[264,256]{1,0:T(8,128)(2,1)S(1)} %get-tuple-element.47), channel_id=1, source_target_pairs={{0,4},{1,5},{2,6},{3,7},{4,0},{5,1},{6,2},{7,3},{8,12},{9,13},{10,... | collective-permute-start | bytes 405512 | tf_op jit(solution)/shard_map/ppermute | solution.py:444
  31.1 6.5 %collective-permute-start.11 = (bf16[264,256]{1,0:T(8,128)(2,1)S(1)}, bf16[264,256]{1,0:T(8,128)(2,1)S(1)}, u32[]{:S(2)}, u32[]{:S(2)}) collective-permute-start(bf16[264,256]{1,0:T(8,128)(2,1)S(1)} %get-tuple-element.48), channel_id=1, source_target_pairs={{0,6},{1,7},{2,4},{3,5},{4,2},{5,3},{6,0},{7,1},{8,14},{9,15},{10,... | collective-permute-start | bytes 405512 | tf_op jit(solution)/shard_map/ppermute | solution.py:444
  37.8 7.0 %collective-permute-start.12 = (bf16[264,256]{1,0:T(8,128)(2,1)S(1)}, bf16[264,256]{1,0:T(8,128)(2,1)S(1)}, u32[]{:S(2)}, u32[]{:S(2)}) collective-permute-start(bf16[264,256]{1,0:T(8,128)(2,1)S(1)} %shard_map.89), channel_id=1, source_target_pairs={{0,24},{8,16},{16,8},{24,0},{1,25},{9,17},{17,9},{25,1},{2,26},{10... | collective-permute-start | bytes 405512 | tf_op jit(solution)/shard_map/ppermute | solution.py:441
  39.8 6.1 %collective-permute-start.5 = (bf16[264,256]{1,0:T(8,128)(2,1)S(1)}, bf16[264,256]{1,0:T(8,128)(2,1)S(1)}, u32[]{:S(2)}, u32[]{:S(2)}) collective-permute-start(bf16[264,256]{1,0:T(8,128)(2,1)S(1)} %get-tuple-element.41), channel_id=1, source_target_pairs={{0,2},{1,3},{2,0},{3,1},{4,6},{5,7},{6,4},{7,5},{8,10},{9,11},{10,... | collective-permute-start | bytes 405512 | tf_op jit(solution)/shard_map/ppermute | solution.py:444
  41.3 7.1 %collective-permute-start.6 = (bf16[264,256]{1,0:T(8,128)(2,1)S(1)}, bf16[264,256]{1,0:T(8,128)(2,1)S(1)}, u32[]{:S(2)}, u32[]{:S(2)}) collective-permute-start(bf16[264,256]{1,0:T(8,128)(2,1)S(1)} %get-tuple-element.42), channel_id=1, source_target_pairs={{0,4},{1,5},{2,6},{3,7},{4,0},{5,1},{6,2},{7,3},{8,12},{9,13},{10,... | collective-permute-start | bytes 405512 | tf_op jit(solution)/shard_map/ppermute | solution.py:444
  41.9 6.5 %collective-permute-start.7 = (bf16[264,256]{1,0:T(8,128)(2,1)S(1)}, bf16[264,256]{1,0:T(8,128)(2,1)S(1)}, u32[]{:S(2)}, u32[]{:S(2)}) collective-permute-start(bf16[264,256]{1,0:T(8,128)(2,1)S(1)} %get-tuple-element.43), channel_id=1, source_target_pairs={{0,6},{1,7},{2,4},{3,5},{4,2},{5,3},{6,0},{7,1},{8,14},{9,15},{10,... | collective-permute-start | bytes 405512 | tf_op jit(solution)/shard_map/ppermute | solution.py:444
